TPU v7x, 256 devices: a whole 4x4x8 slice. The times are simulated.
256 devices in a mesh: gx: 16 (over z, core), gy: 16 (over x, y).
Axes of the slice: x: 4, y: 4, z: 8, core: 2. Of those that a mesh axis runs over, the one named last changes fastest.
Arguments:
- positions: float32 [3, 32, 128, 128], P(None, 'gx', 'gy'), may hold values from 0 to 1
- embed: bfloat16 [32, 128, 128, 256], P('gx', 'gy'), may hold values from -0.75 to 0.75
- counts: int32 [32, 128], P('gx', 'gy'), may hold values from 0 to 128, as said below
- neighbours: int32 [32, 128, 9], P('gx', 'gy'), may hold values from 0 to 40, as said below
- w_one: bfloat16 [256, 256], replicated, may hold values from -0.375 to 0.375
- bias_one: float32 [256], replicated, may hold values from -4 to 4
- w_two: bfloat16 [256, 256], replicated, may hold values from -0.375 to 0.375
- w_out: float32 [256], replicated, may hold values from -0.375 to 0.375
Outputs:
- forces: float32 [3, 32, 128, 128], P(None, 'gx', 'gy')
- energies: float32 [32, 128, 128], P('gx', 'gy')
Inputs may be any that keep to these rules, and one draw needn't show every extreme that they name: `counts`: each device's block of 2 x 8 bins has at most 16 non-empty bins, and some devices have exactly 16. The number of non-empty bins of every device's block is a multiple of the size of gy. The blocks of all devices that share a gx index hold together at most 10 times the size of gy non-empty bins, and some such row holds exactly that many. `neighbours`: entry k of a bin at (x, y) of its device's block is 40 or (x + k // 3) * 10 + y + k % 3, the bin offset by (k // 3 - 1, k % 3 - 1) in the block extended by one ghost bin on every side; entry 4 is always present.
All inputs are finite; a program needn't handle non-finite values.
Results may differ from a plain program's by a relative error of at most 0.014.
Values may be sent and summed in bfloat16 or wider, within the bound.
A program may use at most 64 MiB of HBM per device.

v0:
```python
import jax
import jax.numpy as jnp
from jax import lax
from jax.sharding import PartitionSpec as P

radius = 0.4


def padded(value, sides, width):
    for axis, dim in sides:
        count, length = (lax.axis_size(axis), value.shape[dim])
        up = [(i, (i + 1) % count) for i in range(count)]
        down = [(j, i) for i, j in up]
        last = lax.slice_in_dim(value, length - width, length, axis=dim)
        leading = lax.slice_in_dim(value, 0, width, axis=dim)
        before = lax.ppermute(last, axis, up)
        after = lax.ppermute(leading, axis, down)
        value = jnp.concatenate([before, value, after], axis=dim)
    return value


def shifted(block, axis, distance):
    devices = range(lax.axis_size(axis))
    route = [((i - distance) % len(devices), i) for i in devices]
    return lax.ppermute(block, axis, route)


def network(features, w_one, bias_one, w_two, w_out):
    flat_rows = features.reshape(-1, features.shape[-1])
    act_one = jnp.tanh(jnp.dot(flat_rows, w_one, preferred_element_type=jnp.float32) + bias_one)
    act_two = jnp.tanh(
        jnp.dot(act_one.astype(jnp.bfloat16), w_two, preferred_element_type=jnp.float32)
    )
    energy = jnp.sum(act_two * w_out, axis=-1)
    back_two = (w_out * (1.0 - act_two * act_two)).astype(jnp.bfloat16)
    back_one = (
        jnp.dot(back_two, w_two.T, preferred_element_type=jnp.float32) * (1.0 - act_one * act_one)
    ).astype(jnp.bfloat16)
    gradients = jnp.dot(back_one, w_one.T, preferred_element_type=jnp.float32).astype(jnp.bfloat16)
    return (gradients.reshape(features.shape), energy.reshape(features.shape[:-1]))


def pair_weights(own_pos, own_mask, remote_pos, remote_mask, shift_x, shift_y):
    delta_x = shift_x[:, None, None] + remote_pos[0][:, None, :] - own_pos[0][:, :, None]
    delta_y = shift_y[:, None, None] + remote_pos[1][:, None, :] - own_pos[1][:, :, None]
    delta_z = remote_pos[2][:, None, :] - own_pos[2][:, :, None]
    square = delta_x * delta_x + delta_y * delta_y + delta_z * delta_z
    weight = (
        jnp.exp(-square / (2.0 * radius * radius)) * own_mask[:, :, None] * remote_mask[:, None, :]
    )
    return (weight, delta_x, delta_y, delta_z)


def body(positions, embed, counts, neighbours, w_one, bias_one, w_two, w_out):
    per_bin = positions.shape[-1]
    rows_x, rows_y = counts.shape
    bin_count = rows_x * rows_y
    feat_width = embed.shape[-1]
    atom_index = jnp.arange(per_bin, dtype=jnp.int32)
    occupied = (atom_index[None, None, :] < counts[:, :, None]).astype(jnp.float32)
    coords = jnp.concatenate([positions, occupied[None]], axis=0)
    ext_coords = padded(coords.astype(jnp.bfloat16), (("gx", 1), ("gy", 2)), 1).astype(coords.dtype)
    ext_embed = padded(embed, (("gx", 0), ("gy", 1)), 1)
    ext_cols = rows_y + 2
    extent = (rows_x + 2) * ext_cols
    flat_coords = jnp.concatenate(
        [ext_coords.reshape(4, extent, per_bin), jnp.zeros((4, 1, per_bin), jnp.float32)], axis=1
    )
    flat_embed = jnp.concatenate(
        [
            ext_embed.reshape(extent, per_bin, feat_width),
            jnp.zeros((1, per_bin, feat_width), embed.dtype),
        ],
        axis=0,
    )
    own_pos = positions.reshape(3, bin_count, per_bin)
    own_mask = occupied.reshape(bin_count, per_bin)
    bin_index = jnp.arange(bin_count, dtype=jnp.int32)
    home_x = bin_index // rows_y
    home_y = bin_index % rows_y
    own_slot = (home_x + 1) * ext_cols + home_y + 1
    links = neighbours.reshape(bin_count, 9)

    def gather_bin(neighbour):
        linked = links[:, neighbour]
        shift_x = (linked // ext_cols - home_x - 1).astype(jnp.float32)
        shift_y = (linked % ext_cols - home_y - 1).astype(jnp.float32)
        remote = flat_coords[:, linked]
        return (remote[:3], remote[3], flat_embed[linked], shift_x, shift_y, linked)

    summed = jnp.zeros((bin_count, per_bin, feat_width), jnp.float32)
    for neighbour in range(9):
        remote_pos, remote_mask, remote_embed, shift_x, shift_y, linked = gather_bin(neighbour)
        weight, delta_x, delta_y, delta_z = pair_weights(
            own_pos, own_mask, remote_pos, remote_mask, shift_x, shift_y
        )
        summed = summed + jnp.einsum(
            "bij,bjf->bif",
            weight.astype(jnp.bfloat16),
            remote_embed,
            preferred_element_type=jnp.float32,
        )
    features = summed.astype(jnp.bfloat16)
    gradients, energy = network(features, w_one, bias_one, w_two, w_out)
    ghost_force = jnp.zeros((3, extent + 1, per_bin), jnp.float32)
    own_force = jnp.zeros((3, bin_count, per_bin), jnp.float32)
    for neighbour in range(9):
        remote_pos, remote_mask, remote_embed, shift_x, shift_y, linked = gather_bin(neighbour)
        weight, delta_x, delta_y, delta_z = pair_weights(
            own_pos, own_mask, remote_pos, remote_mask, shift_x, shift_y
        )
        projected = jnp.einsum(
            "bif,bjf->bij", gradients, remote_embed, preferred_element_type=jnp.float32
        )
        strength = projected * weight / (radius * radius)
        moved = [strength * delta_x, strength * delta_y, strength * delta_z]
        own_force = own_force - jnp.stack([jnp.sum(part, axis=2) for part in moved])
        pushed = jnp.stack([jnp.sum(part, axis=1) for part in moved])
        ghost_force = ghost_force.at[:, linked].add(pushed)
    ghost_force = ghost_force.at[:, own_slot].add(own_force)
    grid = ghost_force[:, :extent].reshape(3, rows_x + 2, ext_cols, per_bin)
    from_below = shifted(grid[:, rows_x + 1], "gx", 1)
    from_above = shifted(grid[:, 0], "gx", -1)
    middle = grid[:, 1 : rows_x + 1]
    middle = middle.at[:, 0].add(from_below).at[:, rows_x - 1].add(from_above)
    col_below = shifted(middle[:, :, ext_cols - 1], "gy", 1)
    col_above = shifted(middle[:, :, 0], "gy", -1)
    forces = middle[:, :, 1 : rows_y + 1]
    forces = forces.at[:, :, 0].add(col_below).at[:, :, rows_y - 1].add(col_above)
    return (forces, energy.reshape(rows_x, rows_y, per_bin) * occupied)


def solution(mesh):
    in_specs = (
        P(None, "gx", "gy", None),
        P("gx", "gy", None, None),
        P("gx", "gy"),
        P("gx", "gy", None),
        P(),
        P(),
        P(),
        P(),
    )
    out_specs = (P(None, "gx", "gy", None), P("gx", "gy", None))
    return jax.shard_map(body, mesh=mesh, in_specs=in_specs, out_specs=out_specs, check_vma=False)
```

profile of v0, /device:TPU:1, one launch (start us, length us, event | category | flops | bytes accessed | tf_op | source)
XLA Modules:
  0.0 154.6 jit_solution(4349202112764708513)
XLA Ops:
  2.2 3.0 %collective-permute-start = (bf16[4,1,8,128]{3,2,1,0:T(8,128)(2,1)S(1)}, bf16[4,1,8,128]{3,2,1,0:T(8,128)(2,1)S(1)}, u32[]{:S(2)}, u32[]{:S(2)}) collective-permute-start(bf16[4,1,8,128]{3,2,1,0:T(8,128)(2,1)S(1)} %get-tuple-element.225), channel_id=1, source_target_pairs={{0,16},{16,32},{32,48},{48,64},{64,80},{80,96},{96,112},{112,128},... | collective-permute-start | bytes 24584 | tf_op jit(solution)/shard_map/ppermute | solution.py:16
  5.5 1.3 fusion.296
  6.8 3.6 %collective-permute-start.5 = (bf16[1,8,128,256]{3,2,1,0:T(8,128)(2,1)S(1)}, bf16[1,8,128,256]{3,2,1,0:T(8,128)(2,1)S(1)}, u32[]{:S(2)}, u32[]{:S(2)}) collective-permute-start(bf16[1,8,128,256]{3,2,1,0:T(8,128)(2,1)S(1)} %get-tuple-element.178), channel_id=1, source_target_pairs={{16,0},{32,16},{48,32},{64,48},{80,64},{96,80},{112,96},{128,112},... | collective-permute-start | bytes 1572872 | tf_op jit(solution)/shard_map/ppermute | solution.py:17
  15.7 1.4 collective-permute-start.2
  17.1 3.7 %collective-permute-start.3 = (bf16[4,4,1,128]{3,2,1,0:T(2,128)(2,1)S(1)}, bf16[4,4,1,128]{3,2,1,0:T(2,128)(2,1)S(1)}, u32[]{:S(2)}, u32[]{:S(2)}) collective-permute-start(bf16[4,4,1,128]{3,2,1,0:T(2,128)(2,1)S(1)} %get-tuple-element.219), channel_id=1, source_target_pairs={{1,0},{2,1},{3,2},{4,3},{5,4},{6,5},{7,6},{8,7},{9,8},{10,9},{11,1... | collective-permute-start | bytes 12296 | tf_op jit(solution)/shard_map/ppermute | solution.py:17
  38.3 1.4 broadcast_add_fusion.13
  39.6 1.3 broadcast_add_fusion.12
  44.5 1.3 broadcast_add_fusion.5
  46.1 5.0 %collective-permute-start.7 = (bf16[4,1,128,256]{3,2,1,0:T(8,128)(2,1)S(1)}, bf16[4,1,128,256]{3,2,1,0:T(8,128)(2,1)S(1)}, u32[]{:S(2)}, u32[]{:S(2)}) collective-permute-start(bf16[4,1,128,256]{3,2,1,0:T(8,128)(2,1)S(1)} %get-tuple-element.177), channel_id=1, source_target_pairs={{1,0},{2,1},{3,2},{4,3},{5,4},{6,5},{7,6},{8,7},{9,8},{10,9},{11,1... | collective-permute-start | bytes 786440 | tf_op jit(solution)/shard_map/ppermute | solution.py:17
  51.2 4.6 %collective-permute-done.6 = bf16[4,1,128,256]{3,2,1,0:T(8,128)(2,1)S(1)} collective-permute-done((bf16[4,1,128,256]{3,2,1,0:T(8,128)(2,1)S(1)}, bf16[4,1,128,256]{3,2,1,0:T(8,128)(2,1)S(1)}, u32[]{:S(2)}, u32[]{:S(2)}) %collective-permute-start.6) | collective-permute-done | bytes 262176 | tf_op jit(solution)/shard_map/ppermute | solution.py:16
  56.5 1.7 %gather_fusion.17 = bf16[16,128,256]{2,1,0:T(8,128)(2,1)} fusion(bf16[41,128,256]{2,1,0:T(8,128)(2,1)S(1)} %concatenate.39, s32[1024]{0:T(1024)} %copy-done.71), kind=kCustom, calls=%fused_computation.17 | custom fusion | bytes 2097216 | tf_op jit(solution)/shard_map/gather | solution.py:89
  58.2 1.7 %gather_fusion.15 = bf16[16,128,256]{2,1,0:T(8,128)(2,1)} fusion(bf16[41,128,256]{2,1,0:T(8,128)(2,1)S(1)} %concatenate.39, s32[1024]{0:T(1024)} %pad_clamp_fusion.1), kind=kCustom, calls=%fused_computation.15 | custom fusion | bytes 2097216 | tf_op jit(solution)/shard_map/gather | solution.py:89
  59.9 1.7 %gather_fusion.13 = bf16[16,128,256]{2,1,0:T(8,128)(2,1)} fusion(bf16[41,128,256]{2,1,0:T(8,128)(2,1)S(1)} %concatenate.39, s32[1024]{0:T(1024)} %pad_clamp_fusion.2), kind=kCustom, calls=%fused_computation.13 | custom fusion | bytes 2097216 | tf_op jit(solution)/shard_map/gather | solution.py:89
  61.6 1.7 %gather_fusion.11 = bf16[16,128,256]{2,1,0:T(8,128)(2,1)} fusion(bf16[41,128,256]{2,1,0:T(8,128)(2,1)S(1)} %concatenate.39, s32[1024]{0:T(1024)} %copy-done.70), kind=kCustom, calls=%fused_computation.11 | custom fusion | bytes 2097216 | tf_op jit(solution)/shard_map/gather | solution.py:89
  63.3 1.8 %gather_fusion.9 = bf16[16,128,256]{2,1,0:T(8,128)(2,1)} fusion(bf16[41,128,256]{2,1,0:T(8,128)(2,1)S(1)} %concatenate.39, s32[1024]{0:T(1024)} %copy-done.67), kind=kCustom, calls=%fused_computation.9 | custom fusion | bytes 2097216 | tf_op jit(solution)/shard_map/gather | solution.py:89
  65.1 1.7 %gather_fusion.7 = bf16[16,128,256]{2,1,0:T(8,128)(2,1)} fusion(bf16[41,128,256]{2,1,0:T(8,128)(2,1)S(1)} %concatenate.39, s32[1024]{0:T(1024)} %copy-done.69), kind=kCustom, calls=%fused_computation.7 | custom fusion | bytes 2097216 | tf_op jit(solution)/shard_map/gather | solution.py:89
  66.8 1.7 %gather_fusion.5 = bf16[16,128,256]{2,1,0:T(8,128)(2,1)} fusion(bf16[41,128,256]{2,1,0:T(8,128)(2,1)S(1)} %concatenate.39, s32[1024]{0:T(1024)} %copy-done.66), kind=kCustom, calls=%fused_computation.5 | custom fusion | bytes 2097216 | tf_op jit(solution)/shard_map/gather | solution.py:89
  68.6 1.9 %gather_fusion.3 = bf16[16,128,256]{2,1,0:T(8,128)(2,1)} fusion(bf16[41,128,256]{2,1,0:T(8,128)(2,1)S(1)} %concatenate.39, s32[1024]{0:T(1024)} %copy-done.68), kind=kCustom, calls=%fused_computation.3 | custom fusion | bytes 2097216 | tf_op jit(solution)/shard_map/gather | solution.py:89
  70.5 1.6 %gather_fusion.1 = bf16[16,128,256]{2,1,0:T(8,128)(2,1)} fusion(bf16[41,128,256]{2,1,0:T(8,128)(2,1)S(1)} %concatenate.39, s32[1024]{0:T(1024)S(1)} %pad_clamp_fusion.8), kind=kCustom, calls=%fused_computation.1 | custom fusion | bytes 2097216 | tf_op jit(solution)/shard_map/gather | solution.py:89
  72.1 2.9 %fusion.142 = f32[16,128,256]{2,1,0:T(8,128)S(1)} fusion(bf16[16,128,256]{2,1,0:T(8,128)(2,1)} %gather_fusion.1, f32[16,128]{1,0:T(8,128)S(1)} %bitcast.479, f32[16,128]{1,0:T(8,128)S(1)} %fusion.251, f32[16,128]{1,0:T(8,128)S(1)} %get-tuple-element.223, f32[16,128]{1,0:T(8,128)S(1)} %bitcast.471, f32[16,128]{1,0:T(8,128)S(1)} %get-tuple-element.224, ...), kind=kOutput, calls=%fused_computation.239 | convolution fusion | flops 137625600 | bytes 3211264 | tf_op jit(solution)/shard_map/bij,bjf->bif/dot_general | solution.py:97
  75.1 2.7 %fusion.144 = f32[16,128,256]{2,1,0:T(8,128)S(1)} fusion(bf16[16,128,256]{2,1,0:T(8,128)(2,1)S(1)} %copy-done.6, f32[16,128]{1,0:T(8,128)S(1)} %bitcast.477, f32[16,128]{1,0:T(8,128)S(1)} %bitcast.468, f32[16,128]{1,0:T(8,128)S(1)} %broadcast_add_fusion.14, f32[16,128]{1,0:T(8,128)S(1)} %broadcast_add_fusion.15, f32[16,128]{1,0:T(8,128)S(1)} %fusion.251, ...), kind=kOutput, calls=%fused_computation.240 | convolution fusion | flops 137625600 | bytes 3211264 | tf_op jit(solution)/shard_map/bij,bjf->bif/dot_general | solution.py:97
  77.8 2.7 %fusion.146 = f32[16,128,256]{2,1,0:T(8,128)S(1)} fusion(bf16[16,128,256]{2,1,0:T(8,128)(2,1)S(1)} %copy-done.8, f32[16,128]{1,0:T(8,128)S(1)} %bitcast.483, f32[16,128]{1,0:T(8,128)S(1)} %bitcast.474, f32[16,128]{1,0:T(8,128)S(1)} %copy-done.32, f32[16,128]{1,0:T(8,128)S(1)} %copy-done.30, f32[16,128]{1,0:T(8,128)S(1)} %fusion.251, ...), kind=kOutput, calls=%fused_computation.241 | convolution fusion | flops 137625600 | bytes 3211264 | tf_op jit(solution)/shard_map/bij,bjf->bif/dot_general | solution.py:97
  80.6 2.7 %fusion.148 = f32[16,128,256]{2,1,0:T(8,128)S(1)} fusion(bf16[16,128,256]{2,1,0:T(8,128)(2,1)S(1)} %copy-done.10, f32[16,128]{1,0:T(8,128)S(1)} %bitcast.481, f32[16,128]{1,0:T(8,128)S(1)} %bitcast.455, f32[16,128]{1,0:T(8,128)S(1)} %broadcast_add_fusion.10, f32[16,128]{1,0:T(8,128)S(1)} %broadcast_add_fusion.11, f32[16,128]{1,0:T(8,128)S(1)} %fusion.251, ...), kind=kOutput, calls=%fused_computation.242 | convolution fusion | flops 137625600 | bytes 3211264 | tf_op jit(solution)/shard_map/bij,bjf->bif/dot_general | solution.py:97
  83.4 2.7 %fusion.150 = f32[16,128,256]{2,1,0:T(8,128)S(1)} fusion(bf16[16,128,256]{2,1,0:T(8,128)(2,1)S(1)} %copy-done.12, f32[16,128]{1,0:T(8,128)S(1)} %bitcast.487, f32[16,128]{1,0:T(8,128)S(1)} %bitcast.461, f32[16,128]{1,0:T(8,128)S(1)} %broadcast_add_fusion.8, f32[16,128]{1,0:T(8,128)S(1)} %broadcast_add_fusion.9, f32[16,128]{1,0:T(8,128)S(1)} %fusion.251, ...), kind=kOutput, calls=%fused_computation.243 | convolution fusion | flops 137625600 | bytes 3211264 | tf_op jit(solution)/shard_map/bij,bjf->bif/dot_general | solution.py:97
  86.2 2.7 %fusion.152 = f32[16,128,256]{2,1,0:T(8,128)S(1)} fusion(bf16[16,128,256]{2,1,0:T(8,128)(2,1)S(1)} %copy-done.14, f32[16,128]{1,0:T(8,128)S(1)} %bitcast.485, f32[16,128]{1,0:T(8,128)S(1)} %bitcast.458, f32[16,128]{1,0:T(8,128)S(1)} %broadcast_add_fusion.6, f32[16,128]{1,0:T(8,128)S(1)} %broadcast_add_fusion.7, f32[16,128]{1,0:T(8,128)S(1)} %fusion.251, ...), kind=kOutput, calls=%fused_computation.244 | convolution fusion | flops 137625600 | bytes 3211264 | tf_op jit(solution)/shard_map/bij,bjf->bif/dot_general | solution.py:97
  89.0 2.7 %fusion.154 = f32[16,128,256]{2,1,0:T(8,128)S(1)} fusion(bf16[16,128,256]{2,1,0:T(8,128)(2,1)S(1)} %copy-done.16, f32[16,128]{1,0:T(8,128)S(1)} %bitcast.492, f32[16,128]{1,0:T(8,128)S(1)} %bitcast.490, f32[16,128]{1,0:T(8,128)S(1)} %broadcast_add_fusion.4, f32[16,128]{1,0:T(8,128)S(1)} %copy-done.34, f32[16,128]{1,0:T(8,128)S(1)} %fusion.251, ...), kind=kOutput, calls=%fused_computation.245 | convolution fusion | flops 137625600 | bytes 3211264 | tf_op jit(solution)/shard_map/bij,bjf->bif/dot_general | solution.py:97
  91.7 2.7 %fusion.156 = f32[16,128,256]{2,1,0:T(8,128)S(1)} fusion(bf16[16,128,256]{2,1,0:T(8,128)(2,1)S(1)} %copy-done.3, f32[16,128]{1,0:T(8,128)S(1)} %bitcast.466, f32[16,128]{1,0:T(8,128)S(1)} %bitcast.464, f32[16,128]{1,0:T(8,128)S(1)} %broadcast_add_fusion.2, f32[16,128]{1,0:T(8,128)S(1)} %broadcast_add_fusion.3, f32[16,128]{1,0:T(8,128)S(1)} %fusion.251, ...), kind=kOutput, calls=%fused_computation.246 | convolution fusion | flops 137625600 | bytes 3211264 | tf_op jit(solution)/shard_map/bij,bjf->bif/dot_general | solution.py:97
  94.5 2.0 %add_convert_fusion = bf16[16,128,256]{2,1,0:T(8,128)(2,1)S(1)} fusion(f32[16,128,256]{2,1,0:T(8,128)S(1)} %fusion.156, f32[16,128,256]{2,1,0:T(8,128)S(1)} %fusion.154, f32[16,128,256]{2,1,0:T(8,128)S(1)} %fusion.152, f32[16,128,256]{2,1,0:T(8,128)S(1)} %fusion.150, f32[16,128,256]{2,1,0:T(8,128)S(1)} %fusion.148, f32[16,128,256]{2,1,0:T(8,128)S(1)} %fusion.146, ...), kind=kOutput, calls=%fused_computation.37 | convolution fusion | flops 142344192 | bytes 18939904 | tf_op jit(solution)/shard_map/bij,bjf->bif/dot_general | solution.py:97
  97.1 1.8 %multiply_reduce_fusion = (f32[2048]{0:T(1024)S(1)}, f32[2048,256]{1,0:T(8,128)}) fusion(f32[256]{0:T(256)S(1)} %copy-done.88, bf16[256,256]{1,0:T(8,128)(2,1)S(1)} %copy-done, f32[2048,256]{1,0:T(8,128)S(1)} %fusion), kind=kOutput, calls=%fused_computation.35 | convolution fusion | flops 270006272 | bytes 4334592 | tf_op jit(solution)/shard_map/dot_general | solution.py:32
  99.0 3.4 %convolution_convert_fusion = bf16[2048,256]{1,0:T(8,128)(2,1)} fusion(bf16[256,256]{1,0:T(8,128)(2,1)S(1)} %copy-done.19, bf16[256,256]{1,0:T(8,128)(2,1)S(1)} %copy-done, f32[2048,256]{1,0:T(8,128)S(1)} %fusion, f32[2048,256]{1,0:T(8,128)} %get-tuple-element.255, f32[256]{0:T(256)S(1)} %copy-done.88), kind=kOutput, calls=%fused_computation.34 | convolution fusion | flops 541589504 | bytes 5506048 | tf_op jit(solution)/shard_map/dot_general | solution.py:39
  102.4 3.7 %fusion.115 = (f32[16,128]{1,0:T(8,128)S(1)}, f32[16,128]{1,0:T(8,128)S(1)}, f32[16,128]{1,0:T(8,128)S(1)}, f32[16,128]{1,0:T(8,128)S(1)}, f32[16,128]{1,0:T(8,128)S(1)}, /*index=5*/f32[16,128]{1,0:T(8,128)S(1)}) fusion(f32[16,128]{1,0:T(8,128)} %broadcast_add_fusion.5, f32[16,128]{1,0:T(8,128)S(1)} %get-tuple-element.222, ...), kind=kOutput, calls=%fused_computation.212 | convolution fusion | flops 140234752 | bytes 2211840 | tf_op jit(solution)/shard_map/bif,bjf->bij/dot_general | solution.py:112
  106.2 2.1 %fusion.5 = f32[16,128,128]{2,1,0:T(8,128)} fusion(bf16[16,128,256]{2,1,0:T(8,128)(2,1)S(1)} %bitcast.357, bf16[16,128,256]{2,1,0:T(8,128)(2,1)S(1)} %copy-done.15, f32[16,128]{1,0:T(8,128)S(1)} %bitcast.486, f32[16,128]{1,0:T(8,128)S(1)} %bitcast.459, f32[16,128]{1,0:T(8,128)S(1)} %broadcast_add_fusion.6, f32[16,128]{1,0:T(8,128)S(1)} %broadcast_add_fusion.7, ...), kind=kOutput, calls=%fused_computation.99 | convolution fusion | flops 137887744 | bytes 3211264 | tf_op jit(solution)/shard_map/bif,bjf->bij/dot_general | solution.py:112
  108.4 2.1 %fusion.6 = f32[16,128,128]{2,1,0:T(8,128)} fusion(bf16[16,128,256]{2,1,0:T(8,128)(2,1)S(1)} %bitcast.358, bf16[16,128,256]{2,1,0:T(8,128)(2,1)S(1)} %copy-done.13, f32[16,128]{1,0:T(8,128)S(1)} %bitcast.488, f32[16,128]{1,0:T(8,128)S(1)} %bitcast.462, f32[16,128]{1,0:T(8,128)S(1)} %broadcast_add_fusion.8, f32[16,128]{1,0:T(8,128)S(1)} %broadcast_add_fusion.9, ...), kind=kOutput, calls=%fused_computation.101 | convolution fusion | flops 137887744 | bytes 3211264 | tf_op jit(solution)/shard_map/bif,bjf->bij/dot_general | solution.py:112
  110.6 2.1 %fusion.7 = f32[16,128,128]{2,1,0:T(8,128)} fusion(bf16[16,128,256]{2,1,0:T(8,128)(2,1)S(1)} %bitcast.359, bf16[16,128,256]{2,1,0:T(8,128)(2,1)S(1)} %copy-done.11, f32[16,128]{1,0:T(8,128)S(1)} %bitcast.482, f32[16,128]{1,0:T(8,128)S(1)} %bitcast.456, f32[16,128]{1,0:T(8,128)S(1)} %broadcast_add_fusion.10, f32[16,128]{1,0:T(8,128)S(1)} %broadcast_add_fusion.11, ...), kind=kOutput, calls=%fused_computation.103 | convolution fusion | flops 137887744 | bytes 3211264 | tf_op jit(solution)/shard_map/bif,bjf->bij/dot_general | solution.py:112
  112.8 1.9 %fusion.8 = f32[16,128,128]{2,1,0:T(8,128)S(1)} fusion(bf16[16,128,256]{2,1,0:T(8,128)(2,1)S(1)} %bitcast.360, bf16[16,128,256]{2,1,0:T(8,128)(2,1)S(1)} %copy-done.9, f32[16,128]{1,0:T(8,128)S(1)} %bitcast.484, f32[16,128]{1,0:T(8,128)S(1)} %bitcast.475, f32[16,128]{1,0:T(8,128)S(1)} %copy-done.33, f32[16,128]{1,0:T(8,128)S(1)} %copy-done.31, ...), kind=kOutput, calls=%fused_computation.105 | convolution fusion | flops 137887744 | bytes 3211264 | tf_op jit(solution)/shard_map/bif,bjf->bij/dot_general | solution.py:112
  114.8 1.9 %fusion.9 = f32[16,128,128]{2,1,0:T(8,128)S(1)} fusion(bf16[16,128,256]{2,1,0:T(8,128)(2,1)S(1)} %bitcast.361, bf16[16,128,256]{2,1,0:T(8,128)(2,1)S(1)} %copy-done.7, f32[16,128]{1,0:T(8,128)S(1)} %bitcast.478, f32[16,128]{1,0:T(8,128)S(1)} %bitcast.469, f32[16,128]{1,0:T(8,128)S(1)} %copy-done.25, f32[16,128]{1,0:T(8,128)S(1)} %copy-done.23, ...), kind=kOutput, calls=%fused_computation.107 | convolution fusion | flops 137887744 | bytes 3211264 | tf_op jit(solution)/shard_map/bif,bjf->bij/dot_general | solution.py:112
  116.7 1.9 %fusion.10 = f32[16,128,128]{2,1,0:T(8,128)S(1)} fusion(bf16[16,128,256]{2,1,0:T(8,128)(2,1)S(1)} %bitcast.362, bf16[16,128,256]{2,1,0:T(8,128)(2,1)S(1)} %copy-done.5, f32[16,128]{1,0:T(8,128)S(1)} %bitcast.480, f32[16,128]{1,0:T(8,128)S(1)} %fusion.251, f32[16,128]{1,0:T(8,128)S(1)} %get-tuple-element.223, f32[16,128]{1,0:T(8,128)S(1)} %bitcast.472, ...), kind=kOutput, calls=%fused_computation.109 | convolution fusion | flops 137887744 | bytes 3211264 | tf_op jit(solution)/shard_map/bif,bjf->bij/dot_general | solution.py:112
  118.7 5.1 %fusion.127 = (f32[16,128]{1,0:T(8,128)S(1)}, f32[16,128]{1,0:T(8,128)S(1)}, f32[16,128]{1,0:T(8,128)S(1)}, f32[16,128]{1,0:T(8,128)S(1)}, f32[16,128]{1,0:T(8,1...) fusion(f32[16,128]{1,0:T(8,128)S(1)} %broadcast_add_fusion.1, ...), kind=kOutput, calls=%fused_computation.224 | convolution fusion | flops 149635072 | bytes 5578752 | tf_op jit(solution)/shard_map/bif,bjf->bij/dot_general | solution.py:112
  123.9 1.1 scatter_fusion
  125.0 1.1 scatter_fusion.1
  126.2 1.3 scatter_fusion.2
  127.6 6.4 %fusion.121 = (f32[16,128]{1,0:T(8,128)S(1)}, f32[16,128]{1,0:T(8,128)S(1)}, f32[16,128]{1,0:T(8,128)S(1)}, f32[16,128]{1,0:T(8,128)S(1)}, f32[16,128]{1,0:T(8,1...) fusion(f32[16,128]{1,0:T(8,128)S(1)} %broadcast_add_fusion.3, ...), kind=kOutput, calls=%fused_computation.218 | convolution fusion | flops 149635072 | bytes 5578752 | tf_op jit(solution)/shard_map/bif,bjf->bij/dot_general | solution.py:112
  134.0 1.1 scatter_fusion.3
  137.5 1.1 scatter_fusion.6
  139.8 1.1 scatter_fusion.8
  142.3 1.9 %collective-permute-start.8 = (f32[3,10,128]{2,0,1:T(4,128)S(1)}, f32[3,10,128]{2,0,1:T(4,128)S(1)}, u32[]{:S(2)}, u32[]{:S(2)}) collective-permute-start(f32[3,10,128]{2,0,1:T(4,128)S(1)} %get-tuple-element.181), channel_id=1, source_target_pairs={{240,0},{0,16},{16,32},{32,48},{48,64},{64,80},{80,96},{96,112},{1... | collective-permute-start | bytes 46088 | tf_op jit(solution)/shard_map/ppermute | solution.py:25
  145.5 1.9 %collective-permute-done.9 = f32[3,10,128]{2,0,1:T(4,128)S(1)} collective-permute-done((f32[3,10,128]{2,0,1:T(4,128)S(1)}, f32[3,10,128]{2,0,1:T(4,128)S(1)}, u32[]{:S(2)}, u32[]{:S(2)}) %collective-permute-start.9) | collective-permute-done | bytes 15392 | tf_op jit(solution)/shard_map/ppermute | solution.py:25
  148.3 4.9 %collective-permute-start.11 = (f32[3,2,128]{2,1,0:T(2,128)S(1)}, f32[3,2,128]{2,1,0:T(2,128)S(1)}, u32[]{:S(2)}, u32[]{:S(2)}) collective-permute-start(f32[3,2,128]{2,1,0:T(2,128)S(1)} %get-tuple-element.220), channel_id=1, source_target_pairs={{1,0},{2,1},{3,2},{4,3},{5,4},{6,5},{7,6},{8,7},{9,8},{10,9},{11,1... | collective-permute-start | bytes 9224 | tf_op jit(solution)/shard_map/ppermute | solution.py:25
  (320 shorter events, 38.3 us)
Async XLA Ops:
  0.6 96.3 %copy-start = (bf16[256,256]{1,0:T(8,128)(2,1)S(1)}, bf16[256,256]{1,0:T(8,128)(2,1)}, u32[]{:S(2)}) copy-start(bf16[256,256]{1,0:T(8,128)(2,1)} %param.22) | copy-start | bytes 393220
  0.6 9.7 %copy-start.89 = (s32[2,8]{1,0:T(2,128)S(1)}, s32[2,8]{1,0:T(2,128)}, u32[]{:S(2)}) copy-start(s32[2,8]{1,0:T(2,128)} %param.18) | copy-start | bytes 196
  0.7 9.8 %copy-start.20 = (f32[3,2,8,128]{3,2,1,0:T(8,128)S(1)}, f32[3,2,8,128]{3,2,1,0:T(8,128)}, u32[]{:S(2)}) copy-start(f32[3,2,8,128]{3,2,1,0:T(8,128)} %param.16) | copy-start | bytes 73732
  0.7 9.8 %copy-start.18 = (s32[2,8,9]{2,1,0:T(8,128)S(1)}, s32[2,8,9]{2,1,0:T(8,128)}, u32[]{:S(2)}) copy-start(s32[2,8,9]{2,1,0:T(8,128)} %param.19) | copy-start | bytes 1732
  2.2 13.5 %collective-permute-start = (bf16[4,1,8,128]{3,2,1,0:T(8,128)(2,1)S(1)}, bf16[4,1,8,128]{3,2,1,0:T(8,128)(2,1)S(1)}, u32[]{:S(2)}, u32[]{:S(2)}) collective-permute-start(bf16[4,1,8,128]{3,2,1,0:T(8,128)(2,1)S(1)} %get-tuple-element.225), channel_id=1, source_target_pairs={{0,16},{16,32},{32,48},{48,64},{64,80},{80,96},{96,112},{112,128},... | collective-permute-start | bytes 24584 | tf_op jit(solution)/shard_map/ppermute | solution.py:16
  5.2 10.4 %collective-permute-start.1 = (bf16[4,1,8,128]{3,2,1,0:T(8,128)(2,1)S(1)}, bf16[4,1,8,128]{3,2,1,0:T(8,128)(2,1)S(1)}, u32[]{:S(2)}, u32[]{:S(2)}) collective-permute-start(bf16[4,1,8,128]{3,2,1,0:T(8,128)(2,1)S(1)} %get-tuple-element.226), channel_id=1, source_target_pairs={{16,0},{32,16},{48,32},{64,48},{80,64},{96,80},{112,96},{128,112},... | collective-permute-start | bytes 24584 | tf_op jit(solution)/shard_map/ppermute | solution.py:17
  6.7 39.1 %copy-start.2 = (bf16[2,8,128,256]{3,2,1,0:T(8,128)(2,1)S(1)}, bf16[2,8,128,256]{3,2,1,0:T(8,128)(2,1)}, u32[]{:S(2)}) copy-start(bf16[2,8,128,256]{3,2,1,0:T(8,128)(2,1)} %param.17) | copy-start | bytes 3145732
  6.8 39.2 %collective-permute-start.5 = (bf16[1,8,128,256]{3,2,1,0:T(8,128)(2,1)S(1)}, bf16[1,8,128,256]{3,2,1,0:T(8,128)(2,1)S(1)}, u32[]{:S(2)}, u32[]{:S(2)}) collective-permute-start(bf16[1,8,128,256]{3,2,1,0:T(8,128)(2,1)S(1)} %get-tuple-element.178), channel_id=1, source_target_pairs={{16,0},{32,16},{48,32},{64,48},{80,64},{96,80},{112,96},{128,112},... | collective-permute-start | bytes 1572872 | tf_op jit(solution)/shard_map/ppermute | solution.py:17
  10.4 35.4 %collective-permute-start.4 = (bf16[1,8,128,256]{3,2,1,0:T(8,128)(2,1)S(1)}, bf16[1,8,128,256]{3,2,1,0:T(8,128)(2,1)S(1)}, u32[]{:S(2)}, u32[]{:S(2)}) collective-permute-start(bf16[1,8,128,256]{3,2,1,0:T(8,128)(2,1)S(1)} %get-tuple-element.179), channel_id=1, source_target_pairs={{0,16},{16,32},{32,48},{48,64},{64,80},{80,96},{96,112},{112,128},... | collective-permute-start | bytes 1572872 | tf_op jit(solution)/shard_map/ppermute | solution.py:16
  10.6 6.5 %copy-start.91 = (s32[16]{0:T(128)}, s32[16]{0:T(128)S(1)}, u32[]{:S(2)}) copy-start(s32[16]{0:T(128)S(1)} %fusion.282) | copy-start | bytes 196
  12.5 10.7 %copy-start.78 = (s32[16]{0:T(128)}, s32[16]{0:T(128)S(1)}, u32[]{:S(2)}) copy-start(s32[16]{0:T(128)S(1)} %get-tuple-element.259) | copy-start | bytes 196
  13.0 10.1 %copy-start.80 = (s32[16]{0:T(128)}, s32[16]{0:T(128)S(1)}, u32[]{:S(2)}) copy-start(s32[16]{0:T(128)S(1)} %get-tuple-element.260) | copy-start | bytes 196
  13.6 8.2 %copy-start.72 = (s32[16]{0:T(128)}, s32[16]{0:T(128)S(1)}, u32[]{:S(2)}) copy-start(s32[16]{0:T(128)S(1)} %get-tuple-element.263) | copy-start | bytes 196
  15.5 13.7 %copy-start.67 = (s32[1024]{0:T(1024)}, s32[1024]{0:T(1024)S(1)}, u32[]{:S(2)}) copy-start(s32[1024]{0:T(1024)S(1)} %pad_clamp_fusion.4) | copy-start | bytes 12292
  15.5 12.5 %copy-start.70 = (s32[1024]{0:T(1024)}, s32[1024]{0:T(1024)S(1)}, u32[]{:S(2)}) copy-start(s32[1024]{0:T(1024)S(1)} %pad_clamp_fusion.3) | copy-start | bytes 12292
  15.6 11.2 %copy-start.66 = (s32[1024]{0:T(1024)}, s32[1024]{0:T(1024)S(1)}, u32[]{:S(2)}) copy-start(s32[1024]{0:T(1024)S(1)} %pad_clamp_fusion.6) | copy-start | bytes 12292
  15.6 11.2 %copy-start.69 = (s32[1024]{0:T(1024)}, s32[1024]{0:T(1024)S(1)}, u32[]{:S(2)}) copy-start(s32[1024]{0:T(1024)S(1)} %pad_clamp_fusion.5) | copy-start | bytes 12292
  15.6 13.6 %copy-start.68 = (s32[1024]{0:T(1024)}, s32[1024]{0:T(1024)S(1)}, u32[]{:S(2)}) copy-start(s32[1024]{0:T(1024)S(1)} %pad_clamp_fusion.7) | copy-start | bytes 12292
  15.7 12.3 %copy-start.71 = (s32[1024]{0:T(1024)}, s32[1024]{0:T(1024)S(1)}, u32[]{:S(2)}) copy-start(s32[1024]{0:T(1024)S(1)} %pad_clamp_fusion) | copy-start | bytes 12292
  15.7 6.0 %collective-permute-start.2 = (bf16[4,4,1,128]{3,2,1,0:T(2,128)(2,1)S(1)}, bf16[4,4,1,128]{3,2,1,0:T(2,128)(2,1)S(1)}, u32[]{:S(2)}, u32[]{:S(2)}) collective-permute-start(bf16[4,4,1,128]{3,2,1,0:T(2,128)(2,1)S(1)} %get-tuple-element.218), channel_id=1, source_target_pairs={{0,1},{1,2},{2,3},{3,4},{4,5},{5,6},{6,7},{7,8},{8,9},{9,10},{10,1... | collective-permute-start | bytes 12296 | tf_op jit(solution)/shard_map/ppermute | solution.py:16
  17.1 4.7 %collective-permute-start.3 = (bf16[4,4,1,128]{3,2,1,0:T(2,128)(2,1)S(1)}, bf16[4,4,1,128]{3,2,1,0:T(2,128)(2,1)S(1)}, u32[]{:S(2)}, u32[]{:S(2)}) collective-permute-start(bf16[4,4,1,128]{3,2,1,0:T(2,128)(2,1)S(1)} %get-tuple-element.219), channel_id=1, source_target_pairs={{1,0},{2,1},{3,2},{4,3},{5,4},{6,5},{7,6},{8,7},{9,8},{10,9},{11,1... | collective-permute-start | bytes 12296 | tf_op jit(solution)/shard_map/ppermute | solution.py:17
  34.6 40.3 %copy-start.22 = (f32[16,128]{1,0:T(8,128)}, f32[16,128]{1,0:T(8,128)S(1)}, u32[]{:S(2)}) copy-start(f32[16,128]{1,0:T(8,128)S(1)} %broadcast_add_fusion.15) | copy-start | bytes 24580
  35.4 39.6 %copy-start.24 = (f32[16,128]{1,0:T(8,128)}, f32[16,128]{1,0:T(8,128)S(1)}, u32[]{:S(2)}) copy-start(f32[16,128]{1,0:T(8,128)S(1)} %broadcast_add_fusion.14) | copy-start | bytes 24580
  36.2 35.9 %copy-start.26 = (f32[16,128]{1,0:T(8,128)}, f32[16,128]{1,0:T(8,128)S(1)}, u32[]{:S(2)}) copy-start(f32[16,128]{1,0:T(8,128)S(1)} %broadcast_add_fusion.17) | copy-start | bytes 24580
  36.8 35.2 %copy-start.28 = (f32[16,128]{1,0:T(8,128)}, f32[16,128]{1,0:T(8,128)S(1)}, u32[]{:S(2)}) copy-start(f32[16,128]{1,0:T(8,128)S(1)} %broadcast_add_fusion.16) | copy-start | bytes 24580
  45.8 5.3 %copy-start.94 = (f32[16]{0:T(128)S(1)}, f32[16]{0:T(128)}, u32[]{:S(2)}) copy-start(f32[16]{0:T(128)} %get-tuple-element.251) | copy-start | bytes 196
  45.8 5.3 %copy-start.93 = (f32[16]{0:T(128)S(1)}, f32[16]{0:T(128)}, u32[]{:S(2)}) copy-start(f32[16]{0:T(128)} %get-tuple-element.264) | copy-start | bytes 196
  46.0 9.8 %collective-permute-start.6 = (bf16[4,1,128,256]{3,2,1,0:T(8,128)(2,1)S(1)}, bf16[4,1,128,256]{3,2,1,0:T(8,128)(2,1)S(1)}, u32[]{:S(2)}, u32[]{:S(2)}) collective-permute-start(bf16[4,1,128,256]{3,2,1,0:T(8,128)(2,1)S(1)} %get-tuple-element.176), channel_id=1, source_target_pairs={{0,1},{1,2},{2,3},{3,4},{4,5},{5,6},{6,7},{7,8},{8,9},{9,10},{10,1... | collective-permute-start | bytes 786440 | tf_op jit(solution)/shard_map/ppermute | solution.py:16
  46.1 9.7 %collective-permute-start.7 = (bf16[4,1,128,256]{3,2,1,0:T(8,128)(2,1)S(1)}, bf16[4,1,128,256]{3,2,1,0:T(8,128)(2,1)S(1)}, u32[]{:S(2)}, u32[]{:S(2)}) collective-permute-start(bf16[4,1,128,256]{3,2,1,0:T(8,128)(2,1)S(1)} %get-tuple-element.177), channel_id=1, source_target_pairs={{1,0},{2,1},{3,2},{4,3},{5,4},{6,5},{7,6},{8,7},{9,8},{10,9},{11,1... | collective-permute-start | bytes 786440 | tf_op jit(solution)/shard_map/ppermute | solution.py:17
  51.1 37.7 %copy-start.35 = (f32[16,128]{1,0:T(8,128)}, f32[16,128]{1,0:T(8,128)S(1)}, u32[]{:S(2)}) copy-start(f32[16,128]{1,0:T(8,128)S(1)} %broadcast_add_fusion.4) | copy-start | bytes 24580
  118.6 5.2 %copy-start.87 = (s32[16]{0:T(128)S(1)}, s32[16]{0:T(128)}, u32[]{:S(2)}) copy-start(s32[16]{0:T(128)} %copy-done.86) | copy-start | bytes 196
  118.6 6.4 %copy-start.83 = (s32[16]{0:T(128)S(1)}, s32[16]{0:T(128)}, u32[]{:S(2)}) copy-start(s32[16]{0:T(128)} %copy-done.82) | copy-start | bytes 196
  118.6 7.5 %copy-start.85 = (s32[16]{0:T(128)S(1)}, s32[16]{0:T(128)}, u32[]{:S(2)}) copy-start(s32[16]{0:T(128)} %copy-done.84) | copy-start | bytes 196
  118.7 8.8 %copy-start.4 = (bf16[16,128,256]{2,1,0:T(8,128)(2,1)S(1)}, bf16[16,128,256]{2,1,0:T(8,128)(2,1)}, u32[]{:S(2)}) copy-start(bf16[16,128,256]{2,1,0:T(8,128)(2,1)} %gather_fusion.15) | copy-start | bytes 3145732
  118.7 8.8 %copy-start.43 = (f32[1,16,128]{2,0,1:T(1,128)S(1)}, f32[1,16,128]{2,0,1:T(1,128)}, u32[]{:S(2)}) copy-start(f32[1,16,128]{2,0,1:T(1,128)} %get-tuple-element.215) | copy-start | bytes 24580
  118.7 8.8 %copy-start.45 = (f32[1,16,128]{2,0,1:T(1,128)S(1)}, f32[1,16,128]{2,0,1:T(1,128)}, u32[]{:S(2)}) copy-start(f32[1,16,128]{2,0,1:T(1,128)} %get-tuple-element.217) | copy-start | bytes 24580
  127.5 6.5 %copy-start.79 = (s32[16]{0:T(128)S(1)}, s32[16]{0:T(128)}, u32[]{:S(2)}) copy-start(s32[16]{0:T(128)} %copy-done.78) | copy-start | bytes 196
  127.5 7.7 %copy-start.81 = (s32[16]{0:T(128)S(1)}, s32[16]{0:T(128)}, u32[]{:S(2)}) copy-start(s32[16]{0:T(128)} %copy-done.80) | copy-start | bytes 196
  127.5 8.8 %copy-start.75 = (s32[16]{0:T(128)S(1)}, s32[16]{0:T(128)}, u32[]{:S(2)}) copy-start(s32[16]{0:T(128)} %copy-done.74) | copy-start | bytes 196
  127.5 9.9 %copy-start.77 = (s32[16]{0:T(128)S(1)}, s32[16]{0:T(128)}, u32[]{:S(2)}) copy-start(s32[16]{0:T(128)} %copy-done.76) | copy-start | bytes 196
  127.6 11.1 %copy-start.73 = (s32[16]{0:T(128)S(1)}, s32[16]{0:T(128)}, u32[]{:S(2)}) copy-start(s32[16]{0:T(128)} %copy-done.72) | copy-start | bytes 196
  127.6 12.2 %copy-start.92 = (s32[16]{0:T(128)S(1)}, s32[16]{0:T(128)}, u32[]{:S(2)}) copy-start(s32[16]{0:T(128)} %copy-done.91) | copy-start | bytes 196
  127.6 13.5 %copy-start.96 = (s32[16]{0:T(128)S(1)}, s32[16]{0:T(128)}, u32[]{:S(2)}) copy-start(s32[16]{0:T(128)} %fusion.283) | copy-start | bytes 196
  127.6 20.1 %copy-start.90 = (s32[2,8]{1,0:T(2,128)S(1)}, s32[2,8]{1,0:T(2,128)}, u32[]{:S(2)}) copy-start(s32[2,8]{1,0:T(2,128)} %param.18) | copy-start | bytes 196
  142.3 3.2 %collective-permute-start.8 = (f32[3,10,128]{2,0,1:T(4,128)S(1)}, f32[3,10,128]{2,0,1:T(4,128)S(1)}, u32[]{:S(2)}, u32[]{:S(2)}) collective-permute-start(f32[3,10,128]{2,0,1:T(4,128)S(1)} %get-tuple-element.181), channel_id=1, source_target_pairs={{240,0},{0,16},{16,32},{32,48},{48,64},{64,80},{80,96},{96,112},{1... | collective-permute-start | bytes 46088 | tf_op jit(solution)/shard_map/ppermute | solution.py:25
  144.2 3.2 %collective-permute-start.9 = (f32[3,10,128]{2,0,1:T(4,128)S(1)}, f32[3,10,128]{2,0,1:T(4,128)S(1)}, u32[]{:S(2)}, u32[]{:S(2)}) collective-permute-start(f32[3,10,128]{2,0,1:T(4,128)S(1)} %get-tuple-element.180), channel_id=1, source_target_pairs={{16,0},{32,16},{48,32},{64,48},{80,64},{96,80},{112,96},{128,112},... | collective-permute-start | bytes 46088 | tf_op jit(solution)/shard_map/ppermute | solution.py:25
  147.5 5.9 %collective-permute-start.10 = (f32[3,2,128]{2,1,0:T(2,128)S(1)}, f32[3,2,128]{2,1,0:T(2,128)S(1)}, u32[]{:S(2)}, u32[]{:S(2)}) collective-permute-start(f32[3,2,128]{2,1,0:T(2,128)S(1)} %get-tuple-element.221), channel_id=1, source_target_pairs={{15,0},{0,1},{1,2},{2,3},{3,4},{4,5},{5,6},{6,7},{7,8},{8,9},{9,10... | collective-permute-start | bytes 9224 | tf_op jit(solution)/shard_map/ppermute | solution.py:25
  148.3 5.6 %collective-permute-start.11 = (f32[3,2,128]{2,1,0:T(2,128)S(1)}, f32[3,2,128]{2,1,0:T(2,128)S(1)}, u32[]{:S(2)}, u32[]{:S(2)}) collective-permute-start(f32[3,2,128]{2,1,0:T(2,128)S(1)} %get-tuple-element.220), channel_id=1, source_target_pairs={{1,0},{2,1},{3,2},{4,3},{5,4},{6,5},{7,6},{8,7},{9,8},{10,9},{11,1... | collective-permute-start | bytes 9224 | tf_op jit(solution)/shard_map/ppermute | solution.py:25
  (61 other events, 155.4 us)
where the time goes:
time: 157 us; the launch traced here: 155 us
  matrix products  56.7 us (36%)
  other arithmetic  32.5 us (21%)
  local copies, waits for them, and re-layouts  30.2 us (19%)
  starting transfers between devices  24.4 us (16%)
  waiting for transfers between devices  8.24 us (5%)
  between operations  2.44 us (2%)
    dot_general x9, matrix products, body(): jnp.einsum('bif,bjf->bij', gradients, remote_embed, preferred_element_typ...  27.3 us
    dot_general x9, matrix products, body(): jnp.einsum('bij,bjf->bif', weight.astype(jnp.bfloat16), remote_embed, pre...  23.8 us
    gather x9, local copies, waits for them, and re-layouts, gather_bin(): return (remote[:3], remote[3], flat_embed[linked], shift_x, shift_y, linked)  15.6 us
    ppermute x4, starting transfers between devices, padded(): after = lax.ppermute(leading, axis, down)  12.5 us
    scatter-add x9, other arithmetic, body(): ghost_force = ghost_force.at[:, linked].add(pushed)  10.1 us
    add x9, other arithmetic, pair_weights(): shift_x[:, None, None] + remote_pos[0][:, None, :] - own_pos[0][:, :, None]  7.83 us
    ppermute x4, starting transfers between devices, shifted(): return lax.ppermute(block, axis, route)  7.47 us
    add x9, other arithmetic, pair_weights(): shift_y[:, None, None] + remote_pos[1][:, None, :] - own_pos[1][:, :, None]  5.52 us
  transfers between devices with their start and end apart: 12, of which 6 were waited for; matrix products, arithmetic and copies ran while one was open for 21% of the time, Pallas kernels for 0%

commit v1 on v0

v1 whole, which is shorter than its diff:
```python
import functools

import jax
import jax.numpy as jnp
from jax import lax
from jax.experimental import pallas as pl
from jax.experimental.pallas import tpu as pltpu
from jax.sharding import PartitionSpec as P

MESH = pl.DeviceIdType.MESH
F32 = jnp.float32
BF16 = jnp.bfloat16
radius = 0.4
INV = 1.0 / (radius * radius)
KAPPA = 1.4426950408889634 / (2.0 * radius * radius)
OFF = -30000.0
BX, BY, ATOMS, FEAT, HID = 2, 8, 128, 256, 256
EX, EY = BX + 2, BY + 2
GROUPS = BX * BY // 2
DIRS = ((-1, -1), (-1, 1), (1, -1), (1, 1), (0, -1), (0, 1), (-1, 0), (1, 0))


def rim(step, size):
    return pl.ds(1, 1) if step < 0 else pl.ds(size, 1) if step > 0 else pl.ds(1, size)


def ghost(step, size):
    return pl.ds(0, 1) if step < 0 else pl.ds(size + 1, 1) if step > 0 else pl.ds(1, size)


def split3(value):
    high = value.astype(BF16).astype(F32)
    rest = value - high
    middle = rest.astype(BF16).astype(F32)
    return high, middle, rest - middle


def kernel(
    nx, ny,
    pos_hbm, emb_hbm, cnt, nbr, w1_hbm, b1_hbm, w2_hbm, wo_hbm,
    f_out, e_out,
    emb, emb_t, raw, glob, rows, cols, weight, feat, act, grad, sums, ghost_f, recv_f,
    pos, w1, b1, w2, wo, w1_t, w2_t,
    local_sem, p_send, p_recv, e_send, e_recv, f_send, f_recv,
):
    gx, gy = lax.axis_index("gx"), lax.axis_index("gy")

    def peer(dx, dy):
        return (lax.rem(gx + (dx + nx), nx), lax.rem(gy + (dy + ny), ny))

    barrier = pltpu.get_barrier_semaphore()
    for dx, dy in DIRS:
        pl.semaphore_signal(barrier, inc=1, device_id=peer(dx, dy), device_id_type=MESH)

    loads = [
        pltpu.make_async_copy(pos_hbm, pos, local_sem.at[0]),
        pltpu.make_async_copy(emb_hbm, emb.at[pl.ds(1, BX), pl.ds(1, BY)], local_sem.at[1]),
        pltpu.make_async_copy(w1_hbm, w1, local_sem.at[2]),
        pltpu.make_async_copy(b1_hbm, b1, local_sem.at[3]),
        pltpu.make_async_copy(w2_hbm, w2, local_sem.at[4]),
        pltpu.make_async_copy(wo_hbm, wo, local_sem.at[5]),
    ]
    for load in loads:
        load.start()

    def sends(src, dst, send_sem, recv_sem):
        return [
            pltpu.make_async_remote_copy(
                src_ref=src.at[rim(dx, BX), rim(dy, BY)],
                dst_ref=dst.at[ghost(-dx, BX), ghost(-dy, BY)],
                send_sem=send_sem.at[i],
                recv_sem=recv_sem.at[i],
                device_id=peer(dx, dy),
                device_id_type=MESH,
            )
            for i, (dx, dy) in enumerate(DIRS)
        ]

    p_copies = sends(raw, raw, p_send, p_recv)
    e_copies = sends(emb, emb, e_send, e_recv)
    f_copies = [
        pltpu.make_async_remote_copy(
            src_ref=ghost_f.at[ghost(dx, BX), ghost(dy, BY)],
            dst_ref=recv_f.at[ghost(-dx, BX), ghost(-dy, BY)],
            send_sem=f_send.at[i],
            recv_sem=f_recv.at[i],
            device_id=peer(dx, dy),
            device_id_type=MESH,
        )
        for i, (dx, dy) in enumerate(DIRS)
    ]

    loads[0].wait()
    lane = lax.broadcasted_iota(jnp.int32, (1, ATOMS), 1)
    for x in range(BX):
        for y in range(BY):
            tile = jnp.concatenate(
                [pos[c, x, y : y + 1, :] for c in range(3)]
                + [jnp.where(lane < cnt[x, y], 0.0, OFF).astype(F32)]
                + [jnp.zeros((4, ATOMS), F32)],
                axis=0,
            )
            raw[1 + x, 1 + y] = tile

    pl.semaphore_wait(barrier, len(DIRS))
    for copy in p_copies:
        copy.start()
    loads[1].wait()
    for copy in e_copies:
        copy.start()

    row = lax.broadcasted_iota(jnp.int32, (8, ATOMS), 0)
    mark = lax.broadcasted_iota(jnp.int32, (80, ATOMS), 0)

    def make_rows(ex, ey):
        tile = raw[ex, ey]
        place = tile + jnp.where(row == 0, ex - 1.5, jnp.where(row == 1, ey - 5.0, jnp.where(row == 2, -0.5, 0.0)))
        glob[ex, ey] = place
        square = place * place
        bias = place[3:4] - KAPPA * (square[0:1] + square[1:2] + square[2:3])
        full = jnp.where(row < 3, place, jnp.where(row == 3, bias, jnp.where(row == 4, 1.0, 0.0)))
        high, middle, low = split3(full)
        one_hot = jnp.where(mark == ex * EY + ey, 1.0, 0.0)
        rows[ex, ey] = jnp.concatenate([high, middle, low, high, middle, high, one_hot], axis=0).astype(BF16)
        return place, bias

    def make_cols(x, y, place, bias):
        full = jnp.where(row < 3, (2.0 * KAPPA) * place, jnp.where(row == 3, 1.0, jnp.where(row == 4, bias, 0.0)))
        high, middle, low = split3(full)
        present = mark == nbr[x, y, 0]
        for k in range(1, 9):
            present = jnp.logical_or(present, mark == nbr[x, y, k])
        missing = jnp.where(present, 0.0, OFF)
        stack = jnp.concatenate([high, high, high, middle, middle, low, missing], axis=0)
        cols[x, y] = jnp.transpose(stack).astype(BF16)

    def flip(ex, ey):
        emb_t[ex, ey] = jnp.transpose(emb[ex, ey])

    for x in range(BX):
        for y in range(BY):
            place, bias = make_rows(1 + x, 1 + y)
            make_cols(x, y, place, bias)
    for load in loads[2:]:
        load.wait()
    w1_t[...] = jnp.transpose(w1[...])
    w2_t[...] = jnp.transpose(w2[...])
    for x in range(BX):
        for y in range(BY):
            flip(1 + x, 1 + y)
    sums[...] = jnp.zeros_like(sums)

    for copy in p_copies:
        copy.wait_recv()
    for ey in range(EY):
        make_rows(0, ey)
        make_rows(EX - 1, ey)
    for ex in range(1, EX - 1):
        make_rows(ex, 0)
        make_rows(ex, EY - 1)

    def weights_of(g):
        x, y = g // (BY // 2), 2 * (g % (BY // 2))
        left = jnp.concatenate([cols[x, y], cols[x, y + 1]], axis=0)
        for dr in range(3):
            right = jnp.concatenate([rows[x + dr, y + c] for c in range(4)], axis=1)
            power = jnp.dot(left, right, preferred_element_type=F32)
            weight[g, dr] = jnp.exp2(power).astype(BF16)

    for g in range(GROUPS):
        weights_of(g)

    for copy in e_copies:
        copy.wait_recv()
    for ey in range(EY):
        flip(0, ey)
        flip(EX - 1, ey)
    for ex in range(1, EX - 1):
        flip(ex, 0)
        flip(ex, EY - 1)

    def features_of(g):
        x, y = g // (BY // 2), 2 * (g % (BY // 2))
        total = None
        for dr in range(3):
            block = emb[x + dr, pl.ds(y, 4)].reshape(4 * ATOMS, FEAT)
            part = jnp.dot(weight[g, dr], block, preferred_element_type=F32)
            total = part if total is None else total + part
        feat[g] = total.astype(BF16)

    for g in range(GROUPS):
        features_of(g)

    out_row = wo[...]
    bias_row = b1[...]
    for g in range(GROUPS):
        act[g] = jnp.tanh(jnp.dot(feat[g], w1[...], preferred_element_type=F32) + bias_row)
    for g in range(GROUPS):
        x, y = g // (BY // 2), 2 * (g % (BY // 2))
        two = jnp.tanh(jnp.dot(act[g].astype(BF16), w2[...], preferred_element_type=F32))
        scaled = two * out_row
        halves = scaled[:, :128] + scaled[:, 128:]
        for b in range(2):
            turned = jnp.transpose(halves[b * ATOMS : (b + 1) * ATOMS])
            energy = jnp.sum(turned, axis=0, keepdims=True)
            e_out[x, y + b : y + b + 1, :] = jnp.where(lane < cnt[x, y + b], energy, 0.0)
        feat[g] = (out_row * (1.0 - two * two)).astype(BF16)
    for g in range(GROUPS):
        one = act[g]
        back = jnp.dot(feat[g], w2_t[...], preferred_element_type=F32) * (1.0 - one * one)
        grad[g] = jnp.dot(back.astype(BF16), w1_t[...], preferred_element_type=F32).astype(BF16)

    def forces_of(g):
        x, y = g // (BY // 2), 2 * (g % (BY // 2))
        slope = grad[g]
        own = jnp.concatenate([rows[x + 1, y + 1, 0:16], rows[x + 1, y + 2, 0:16]], axis=1)
        total = None
        for dr in range(3):
            right = jnp.concatenate([emb_t[x + dr, y + c] for c in range(4)], axis=1)
            projected = jnp.dot(slope, right, preferred_element_type=F32)
            strength = projected.astype(BF16) * weight[g, dr]
            other = jnp.concatenate([rows[x + dr, y + c, 0:16] for c in range(4)], axis=1)
            part = lax.dot_general(
                strength, other, (((1,), (1,)), ((), ())), preferred_element_type=F32
            )
            total = part if total is None else total + part
            pushed = jnp.dot(own, strength, preferred_element_type=F32)
            for c in range(4):
                sums[x + dr, y + c] += pushed[:, c * ATOMS : (c + 1) * ATOMS]
        turned = jnp.transpose(total)
        for b in range(2):
            sums[x + 1, y + 1 + b] += turned[:, b * ATOMS : (b + 1) * ATOMS]

    for g in range(GROUPS):
        forces_of(g)

    def force_tile(ex, ey):
        moment = sums[ex, ey, 0:8] + sums[ex, ey, 8:16]
        return (glob[ex, ey] * moment[4:5] - moment) * INV

    for ey in range(EY):
        ghost_f[0, ey] = force_tile(0, ey)
        ghost_f[EX - 1, ey] = force_tile(EX - 1, ey)
    for ex in range(1, EX - 1):
        ghost_f[ex, 0] = force_tile(ex, 0)
        ghost_f[ex, EY - 1] = force_tile(ex, EY - 1)
    for x in range(BX):
        for y in range(BY):
            sums[1 + x, 1 + y, 0:8] = force_tile(1 + x, 1 + y)
    for copy in f_copies:
        copy.start()
    for copy in f_copies:
        copy.wait_recv()
    for x in range(BX):
        outer = 0 if x == 0 else EX - 1
        for y in range(BY):
            tile = sums[1 + x, 1 + y, 0:8] + recv_f[outer, 1 + y]
            if y == 0:
                tile = tile + recv_f[1 + x, 0] + recv_f[outer, 0]
            if y == BY - 1:
                tile = tile + recv_f[1 + x, EY - 1] + recv_f[outer, EY - 1]
            for c in range(3):
                f_out[c, x, y : y + 1, :] = tile[c : c + 1]
    for copies in (p_copies, e_copies, f_copies):
        for copy in copies:
            copy.wait_send()


def solution(mesh):
    nx, ny = mesh.shape["gx"], mesh.shape["gy"]

    def body(positions, embed, counts, neighbours, w_one, bias_one, w_two, w_out):
        hbm = pl.BlockSpec(memory_space=pl.ANY)
        smem = pl.BlockSpec(memory_space=pltpu.SMEM)
        vmem = pl.BlockSpec(memory_space=pltpu.VMEM)
        return pl.pallas_call(
            functools.partial(kernel, nx, ny),
            out_shape=(
                jax.ShapeDtypeStruct((3, BX, BY, ATOMS), F32),
                jax.ShapeDtypeStruct((BX, BY, ATOMS), F32),
            ),
            in_specs=[hbm, hbm, smem, smem, hbm, hbm, hbm, hbm],
            out_specs=(vmem, vmem),
            scratch_shapes=[
                pltpu.VMEM((EX, EY, ATOMS, FEAT), BF16),
                pltpu.VMEM((EX, EY, FEAT, ATOMS), BF16),
                pltpu.VMEM((EX, EY, 8, ATOMS), F32),
                pltpu.VMEM((EX, EY, 8, ATOMS), F32),
                pltpu.VMEM((EX, EY, 128, ATOMS), BF16),
                pltpu.VMEM((BX, BY, ATOMS, 128), BF16),
                pltpu.VMEM((GROUPS, 3, 2 * ATOMS, 4 * ATOMS), BF16),
                pltpu.VMEM((GROUPS, 2 * ATOMS, FEAT), BF16),
                pltpu.VMEM((GROUPS, 2 * ATOMS, HID), F32),
                pltpu.VMEM((GROUPS, 2 * ATOMS, FEAT), BF16),
                pltpu.VMEM((EX, EY, 16, ATOMS), F32),
                pltpu.VMEM((EX, EY, 8, ATOMS), F32),
                pltpu.VMEM((EX, EY, 8, ATOMS), F32),
                pltpu.VMEM((3, BX, BY, ATOMS), F32),
                pltpu.VMEM((FEAT, HID), BF16),
                pltpu.VMEM((1, HID), F32),
                pltpu.VMEM((HID, HID), BF16),
                pltpu.VMEM((1, HID), F32),
                pltpu.VMEM((HID, FEAT), BF16),
                pltpu.VMEM((HID, HID), BF16),
                pltpu.SemaphoreType.DMA((6,)),
                pltpu.SemaphoreType.DMA((8,)),
                pltpu.SemaphoreType.DMA((8,)),
                pltpu.SemaphoreType.DMA((8,)),
                pltpu.SemaphoreType.DMA((8,)),
                pltpu.SemaphoreType.DMA((8,)),
                pltpu.SemaphoreType.DMA((8,)),
            ],
            compiler_params=pltpu.CompilerParams(
                collective_id=0, has_side_effects=True, vmem_limit_bytes=60 * 1024 * 1024
            ),
        )(positions, embed, counts, neighbours, w_one, bias_one[None], w_two, w_out[None])

    in_specs = (
        P(None, "gx", "gy", None),
        P("gx", "gy", None, None),
        P("gx", "gy"),
        P("gx", "gy", None),
        P(),
        P(),
        P(),
        P(),
    )
    out_specs = (P(None, "gx", "gy", None), P("gx", "gy", None))
    return jax.shard_map(body, mesh=mesh, in_specs=in_specs, out_specs=out_specs, check_vma=False)
```

time: 157 us -> 37.5 us (0.24); the launches traced: 155 us -> 37.1 us
  matrix products: 56.7 us -> 0 us
  Pallas kernels: 0 us -> 34.5 us
  other arithmetic: 32.5 us -> 0 us
  local copies, waits for them, and re-layouts: 30.2 us -> 1.95 us
  starting transfers between devices: 24.4 us -> 0 us
  waiting for transfers between devices: 8.24 us -> 0 us
  between operations: 2.44 us -> 0.65 us
    dot_general x21 -> x0, matrix products: 56.7 us -> none  [the longest x9 27.3 us: body(): jnp.einsum('bif,bjf->bij', gradients, remote_embed, preferred_element_typ...]
    pallas_call x0 -> x1, Pallas kernels: none -> 34.5 us  [body(): pl.pallas_call(functools.partial(kernel, nx, ny), out_shape=(jax.ShapeDty...]
    ppermute x12 -> x0, starting transfers between devices: 24.4 us -> none  [the longest x4 12.5 us: padded(): after = lax.ppermute(leading, axis, down)]
    gather x18 -> x0, local copies, waits for them, and re-layouts: 21.1 us -> none  [the longest x9 15.6 us: gather_bin(): return (remote[:3], remote[3], flat_embed[linked], shift_x, shift_y, linked)]
    add x20 -> x0, other arithmetic: 13.4 us -> none  [the longest x9 7.83 us: pair_weights(): shift_x[:, None, None] + remote_pos[0][:, None, :] - own_pos[0][:, :, None]]
    scatter-add x12 -> x0, other arithmetic: 11.2 us -> none  [the longest x9 10.1 us: body(): ghost_force = ghost_force.at[:, linked].add(pushed)]
    ppermute x12 -> x0, waiting for transfers between devices: 8.24 us -> none  [the longest x4 4.94 us: padded(): before = lax.ppermute(last, axis, up)]
    slice x15 -> x0, local copies, waits for them, and re-layouts: 6.45 us -> none  [the longest x9 5.02 us: pair_weights(): remote_pos[0][:, None, :]]
  transfers between devices with their start and end apart: 12 -> 0, of which waited for: 6 -> 0; matrix products, arithmetic and copies ran while one was open for 21% -> 0% of each run, Pallas kernels for 0% -> 0%
where the time goes in v1:
time: 37.5 us; the launch traced here: 37.1 us
  Pallas kernels  34.5 us (92%)
  local copies, waits for them, and re-layouts  1.95 us (5%)
  between operations  0.65 us (2%)
    pallas_call x1, Pallas kernels, body(): pl.pallas_call(functools.partial(kernel, nx, ny), out_shape=(jax.ShapeDty...  34.5 us
    unnamed x4, local copies, waits for them, and re-layouts  1.95 us

profile of v1, /device:TPU:1, one launch (start us, length us, event | category | flops | bytes accessed | tf_op | source)
XLA Modules:
  0.0 37.1 jit_solution(6667403344252873824)
XLA Ops:
  0.6 34.5 %shard_map.95 = (f32[3,2,8,128]{3,2,1,0:T(8,128)}, f32[2,8,128]{2,1,0:T(8,128)}) custom-call(f32[3,2,8,128]{3,2,1,0:T(8,128)} %pos_hbm.1, bf16[2,8,128,256]{3,2,1,0:T(8,128)(2,1)} %emb_hbm.1, s32[2,8]{1,0:T(2,128)} %cnt.1, s32[2,8,9]{2,1,0:T(8,128)} %nbr.1, bf16[256,256]{1,0:T(8,128)(2,1)} %w1_hbm.1, f32[1,256]{1,0:T(1,128)} %bitcast.2, ...), custom_call_target="tpu_custom_call" | custom-call | tf_op jit(solution)/shard_map/pallas_call | solution.py:276
  35.1 0.0 copy-start
  35.1 1.4 %copy.12 = f32[3,2,8,128]{3,2,1,0:T(8,128)} copy(f32[3,2,8,128]{3,2,1,0:T(8,128)} %get-tuple-element.4) | data formatting | bytes 49152
  36.5 0.0 copy-done
  36.5 0.6 %copy.13 = f32[2,8,128]{2,1,0:T(8,128)} copy(f32[2,8,128]{2,1,0:T(8,128)S(1)} %copy-done) | data formatting | bytes 16384
Async XLA Ops:
  35.1 1.4 %copy-start = (f32[2,8,128]{2,1,0:T(8,128)S(1)}, f32[2,8,128]{2,1,0:T(8,128)}, u32[]{:S(2)}) copy-start(f32[2,8,128]{2,1,0:T(8,128)} %get-tuple-element.5) | copy-start | bytes 24580

commit v2 on v1

v2 whole, which is shorter than its diff:
```python
import functools

import jax
import jax.numpy as jnp
from jax import lax
from jax.experimental import pallas as pl
from jax.experimental.pallas import tpu as pltpu
from jax.sharding import PartitionSpec as P

MESH = pl.DeviceIdType.MESH
F32 = jnp.float32
BF16 = jnp.bfloat16
radius = 0.4
INV = 1.0 / (radius * radius)
KAPPA = 1.4426950408889634 / (2.0 * radius * radius)
OFF = -30000.0
BX, BY, ATOMS, FEAT, HID = 2, 8, 128, 256, 256
EX, EY = BX + 2, BY + 2
GROUPS = BX * BY // 2
DIRS = ((-1, 0), (-1, -1), (-1, 1), (0, -1), (0, 1), (1, 0), (1, -1), (1, 1))


def rim(step, size):
    return pl.ds(1, 1) if step < 0 else pl.ds(size, 1) if step > 0 else pl.ds(1, size)


def ghost(step, size):
    return pl.ds(0, 1) if step < 0 else pl.ds(size + 1, 1) if step > 0 else pl.ds(1, size)


def split3(value):
    high = value.astype(BF16).astype(F32)
    rest = value - high
    middle = rest.astype(BF16).astype(F32)
    return high, middle, rest - middle


def kernel(
    nx, ny,
    pos_hbm, emb_hbm, cnt, nbr, w1_hbm, b1_hbm, w2_hbm, wo_hbm,
    f_out, e_out,
    emb, emb_t, raw, glob, rows, cols, weight, feat, act, grad, sums, ghost_f, recv_f,
    pos, w1, b1, w2, wo, w1_t, w2_t,
    local_sem, p_send, p_recv, e_send, e_recv, f_send, f_recv,
):
    gx, gy = lax.axis_index("gx"), lax.axis_index("gy")
    odd = lax.rem(gx, 2)
    sign = 1 - 2 * odd
    turn = sign.astype(F32)

    def peer(side, dy):
        return (lax.rem(gx + side * sign + nx, nx), lax.rem(gy + (dy + ny), ny))

    def home(x):
        return x + odd * (1 - 2 * x)

    barrier = pltpu.get_barrier_semaphore()
    for side, dy in DIRS:
        pl.semaphore_signal(barrier, inc=1, device_id=peer(side, dy), device_id_type=MESH)

    loads = [
        pltpu.make_async_copy(pos_hbm, pos, local_sem.at[0]),
        pltpu.make_async_copy(emb_hbm.at[home(0)], emb.at[1, pl.ds(1, BY)], local_sem.at[1]),
        pltpu.make_async_copy(emb_hbm.at[home(1)], emb.at[2, pl.ds(1, BY)], local_sem.at[6]),
        pltpu.make_async_copy(w1_hbm, w1, local_sem.at[2]),
        pltpu.make_async_copy(b1_hbm, b1, local_sem.at[3]),
        pltpu.make_async_copy(w2_hbm, w2, local_sem.at[4]),
        pltpu.make_async_copy(wo_hbm, wo, local_sem.at[5]),
    ]
    for load in loads:
        load.start()

    def send(src, dst, send_sem, recv_sem, i, target):
        return pltpu.make_async_remote_copy(
            src_ref=src, dst_ref=dst, send_sem=send_sem.at[i], recv_sem=recv_sem.at[i],
            device_id=target, device_id_type=MESH,
        )

    p_copies = [
        send(raw.at[rim(side, BX), rim(dy, BY)], raw.at[ghost(side, BX), ghost(-dy, BY)],
             p_send, p_recv, i, peer(side, dy))
        for i, (side, dy) in enumerate(DIRS)
    ]
    f_copies = [
        send(ghost_f.at[ghost(side, BX), ghost(dy, BY)], recv_f.at[ghost(side, BX), ghost(-dy, BY)],
             f_send, f_recv, i, peer(side, dy))
        for i, (side, dy) in enumerate(DIRS)
    ]
    lo, hi, mid, all_y, both = pl.ds(1, 1), pl.ds(BY, 1), pl.ds(2, BY - 2), pl.ds(1, BY), pl.ds(1, BX)
    west, east = pl.ds(0, 1), pl.ds(BY + 1, 1)
    routes = (
        (both, lo, both, east, 0, -1),
        (both, hi, both, west, 0, 1),
        (pl.ds(1, 1), lo, pl.ds(0, 1), lo, -1, 0),
        (pl.ds(1, 1), hi, pl.ds(0, 1), hi, -1, 0),
        (pl.ds(1, 1), mid, pl.ds(0, 1), mid, -1, 0),
        (pl.ds(2, 1), all_y, pl.ds(3, 1), all_y, 1, 0),
        (pl.ds(3, 1), lo, pl.ds(3, 1), east, 0, -1),
        (pl.ds(3, 1), hi, pl.ds(3, 1), west, 0, 1),
        (pl.ds(0, 1), lo, pl.ds(0, 1), east, 0, -1),
        (pl.ds(0, 1), hi, pl.ds(0, 1), west, 0, 1),
    )
    e_copies = [
        send(emb.at[sx, sy], emb.at[tx, ty], e_send, e_recv, i, peer(side, dy))
        for i, (sx, sy, tx, ty, side, dy) in enumerate(routes)
    ]
    cols_in, far_edges, far_mid, near_in = e_copies[0:2], e_copies[2:4], e_copies[4:5], e_copies[5:6]
    near_relay, far_relay = e_copies[6:8], e_copies[8:10]

    def start(copies):
        for copy in copies:
            copy.start()

    def arrive(copies):
        for copy in copies:
            copy.wait_recv()

    loads[0].wait()
    lane = lax.broadcasted_iota(jnp.int32, (1, ATOMS), 1)
    for x in range(BX):
        for y in range(BY):
            tile = jnp.concatenate(
                [pos[c, home(x), y : y + 1, :] for c in range(3)]
                + [jnp.where(lane < cnt[home(x), y], 0.0, OFF).astype(F32)]
                + [jnp.zeros((4, ATOMS), F32)],
                axis=0,
            )
            raw[1 + x, 1 + y] = tile

    pl.semaphore_wait(barrier, len(DIRS))
    start(p_copies)
    loads[1].wait()
    start(far_edges + far_mid)
    loads[2].wait()
    start(near_in + cols_in)

    row = lax.broadcasted_iota(jnp.int32, (8, ATOMS), 0)
    mark = lax.broadcasted_iota(jnp.int32, (80, ATOMS), 0)

    def make_rows(ex, ey):
        tile = raw[ex, ey]
        place = tile + jnp.where(
            row == 0, turn * (ex - 1.5), jnp.where(row == 1, ey - 5.0, jnp.where(row == 2, -0.5, 0.0))
        )
        glob[ex, ey] = place
        square = place * place
        bias = place[3:4] - KAPPA * (square[0:1] + square[1:2] + square[2:3])
        full = jnp.where(row < 3, place, jnp.where(row == 3, bias, jnp.where(row == 4, 1.0, 0.0)))
        high, middle, low = split3(full)
        one_hot = jnp.where(mark == (ex + odd * (EX - 1 - 2 * ex)) * EY + ey, 1.0, 0.0)
        rows[ex, ey] = jnp.concatenate([high, middle, low, high, middle, high, one_hot], axis=0).astype(BF16)
        return place, bias

    def make_cols(x, y, place, bias):
        full = jnp.where(row < 3, (2.0 * KAPPA) * place, jnp.where(row == 3, 1.0, jnp.where(row == 4, bias, 0.0)))
        high, middle, low = split3(full)
        present = mark == nbr[home(x), y, 0]
        for k in range(1, 9):
            present = jnp.logical_or(present, mark == nbr[home(x), y, k])
        missing = jnp.where(present, 0.0, OFF)
        stack = jnp.concatenate([high, high, high, middle, middle, low, missing], axis=0)
        cols[x, y] = jnp.transpose(stack).astype(BF16)

    def flip(ex, ey):
        emb_t[ex, ey] = jnp.transpose(emb[ex, ey])

    for x in range(BX):
        for y in range(BY):
            place, bias = make_rows(1 + x, 1 + y)
            make_cols(x, y, place, bias)
    for load in loads[3:]:
        load.wait()
    w1_t[...] = jnp.transpose(w1[...])
    w2_t[...] = jnp.transpose(w2[...])
    for x in range(BX):
        for y in range(BY):
            flip(1 + x, 1 + y)
    sums[...] = jnp.zeros_like(sums)

    arrive(near_in)
    start(near_relay)
    arrive(p_copies)
    for ey in range(EY):
        make_rows(EX - 1, ey)
        make_rows(0, ey)
    for ex in range(1, EX - 1):
        make_rows(ex, 0)
        make_rows(ex, EY - 1)

    def spot(g):
        return g // (BY // 2), 2 * (g % (BY // 2))

    def weights_of(g):
        x, y = spot(g)
        left = jnp.concatenate([cols[x, y], cols[x, y + 1]], axis=0)
        for dr in range(3):
            right = jnp.concatenate([rows[x + dr, y + c] for c in range(4)], axis=1)
            power = jnp.dot(left, right, preferred_element_type=F32)
            weight[g, dr] = jnp.exp2(power).astype(BF16)

    def features_of(g):
        x, y = spot(g)
        total = None
        for dr in range(3):
            block = emb[x + dr, pl.ds(y, 4)].reshape(4 * ATOMS, FEAT)
            part = jnp.dot(weight[g, dr], block, preferred_element_type=F32)
            total = part if total is None else total + part
        feat[g] = total.astype(BF16)

    out_row = wo[...]
    bias_row = b1[...]

    def network(groups):
        for g in groups:
            act[g] = jnp.tanh(jnp.dot(feat[g], w1[...], preferred_element_type=F32) + bias_row)
        for g in groups:
            x, y = spot(g)
            two = jnp.tanh(jnp.dot(act[g].astype(BF16), w2[...], preferred_element_type=F32))
            scaled = two * out_row
            halves = scaled[:, :128] + scaled[:, 128:]
            for b in range(2):
                turned = jnp.transpose(halves[b * ATOMS : (b + 1) * ATOMS])
                energy = jnp.sum(turned, axis=0, keepdims=True)
                e_out[home(x), y + b : y + b + 1, :] = jnp.where(lane < cnt[home(x), y + b], energy, 0.0)
            feat[g] = (out_row * (1.0 - two * two)).astype(BF16)
        for g in groups:
            one = act[g]
            back = jnp.dot(feat[g], w2_t[...], preferred_element_type=F32) * (1.0 - one * one)
            grad[g] = back.astype(BF16)
        for g in groups:
            grad[g] = jnp.dot(grad[g], w1_t[...], preferred_element_type=F32).astype(BF16)

    def forces_of(g, steps):
        x, y = spot(g)
        slope = grad[g]
        own = jnp.concatenate([rows[x + 1, y + 1, 0:16], rows[x + 1, y + 2, 0:16]], axis=1)
        total = None
        for dr in steps:
            right = jnp.concatenate([emb_t[x + dr, y + c] for c in range(4)], axis=1)
            projected = jnp.dot(slope, right, preferred_element_type=F32)
            strength = projected.astype(BF16) * weight[g, dr]
            other = jnp.concatenate([rows[x + dr, y + c, 0:16] for c in range(4)], axis=1)
            part = lax.dot_general(
                strength, other, (((1,), (1,)), ((), ())), preferred_element_type=F32
            )
            total = part if total is None else total + part
            pushed = jnp.dot(own, strength, preferred_element_type=F32)
            for c in range(4):
                sums[x + dr, y + c] += pushed[:, c * ATOMS : (c + 1) * ATOMS]
        turned = jnp.transpose(total)
        for b in range(2):
            sums[x + 1, y + 1 + b] += turned[:, b * ATOMS : (b + 1) * ATOMS]

    def force_tile(ex, ey):
        moment = sums[ex, ey, 0:8] + sums[ex, ey, 8:16]
        return (glob[ex, ey] * moment[4:5] - moment) * INV

    far, near = range(GROUPS // 2), range(GROUPS // 2, GROUPS)
    for g in near:
        weights_of(g)
    arrive(far_edges)
    start(far_relay)
    for g in far:
        weights_of(g)

    arrive(cols_in + near_relay)
    for ey in range(EY):
        flip(EX - 1, ey)
    for ex in range(1, EX - 1):
        flip(ex, 0)
        flip(ex, EY - 1)
    for g in near:
        features_of(g)
    network(near)
    for g in near:
        forces_of(g, (2, 0, 1))
    for ey in range(EY):
        ghost_f[EX - 1, ey] = force_tile(EX - 1, ey)
    start(f_copies[5:8])

    arrive(far_mid + far_relay)
    for ey in range(EY):
        flip(0, ey)
    for g in far:
        features_of(g)
    network(far)
    for g in far:
        forces_of(g, (0,))
    for ey in range(EY):
        ghost_f[0, ey] = force_tile(0, ey)
    start(f_copies[0:3])
    forces_of(0, (1, 2))
    forces_of(3, (1, 2))
    for ex in range(1, EX - 1):
        ghost_f[ex, 0] = force_tile(ex, 0)
        ghost_f[ex, EY - 1] = force_tile(ex, EY - 1)
    start(f_copies[3:5])
    forces_of(1, (1, 2))
    forces_of(2, (1, 2))
    for x in range(BX):
        for y in range(BY):
            sums[1 + x, 1 + y, 0:8] = force_tile(1 + x, 1 + y)
    arrive(f_copies)
    for x in range(BX):
        outer = 0 if x == 0 else EX - 1
        for y in range(BY):
            tile = sums[1 + x, 1 + y, 0:8] + recv_f[outer, 1 + y]
            if y == 0:
                tile = tile + recv_f[1 + x, 0] + recv_f[outer, 0]
            if y == BY - 1:
                tile = tile + recv_f[1 + x, EY - 1] + recv_f[outer, EY - 1]
            for c in range(3):
                f_out[c, home(x), y : y + 1, :] = tile[c : c + 1]
    for copies in (p_copies, e_copies, f_copies):
        for copy in copies:
            copy.wait_send()


def solution(mesh):
    nx, ny = mesh.shape["gx"], mesh.shape["gy"]

    def body(positions, embed, counts, neighbours, w_one, bias_one, w_two, w_out):
        hbm = pl.BlockSpec(memory_space=pl.ANY)
        smem = pl.BlockSpec(memory_space=pltpu.SMEM)
        vmem = pl.BlockSpec(memory_space=pltpu.VMEM)
        return pl.pallas_call(
            functools.partial(kernel, nx, ny),
            out_shape=(
                jax.ShapeDtypeStruct((3, BX, BY, ATOMS), F32),
                jax.ShapeDtypeStruct((BX, BY, ATOMS), F32),
            ),
            in_specs=[hbm, hbm, smem, smem, hbm, hbm, hbm, hbm],
            out_specs=(vmem, vmem),
            scratch_shapes=[
                pltpu.VMEM((EX, EY, ATOMS, FEAT), BF16),
                pltpu.VMEM((EX, EY, FEAT, ATOMS), BF16),
                pltpu.VMEM((EX, EY, 8, ATOMS), F32),
                pltpu.VMEM((EX, EY, 8, ATOMS), F32),
                pltpu.VMEM((EX, EY, 128, ATOMS), BF16),
                pltpu.VMEM((BX, BY, ATOMS, 128), BF16),
                pltpu.VMEM((GROUPS, 3, 2 * ATOMS, 4 * ATOMS), BF16),
                pltpu.VMEM((GROUPS, 2 * ATOMS, FEAT), BF16),
                pltpu.VMEM((GROUPS, 2 * ATOMS, HID), F32),
                pltpu.VMEM((GROUPS, 2 * ATOMS, FEAT), BF16),
                pltpu.VMEM((EX, EY, 16, ATOMS), F32),
                pltpu.VMEM((EX, EY, 8, ATOMS), F32),
                pltpu.VMEM((EX, EY, 8, ATOMS), F32),
                pltpu.VMEM((3, BX, BY, ATOMS), F32),
                pltpu.VMEM((FEAT, HID), BF16),
                pltpu.VMEM((1, HID), F32),
                pltpu.VMEM((HID, HID), BF16),
                pltpu.VMEM((1, HID), F32),
                pltpu.VMEM((HID, FEAT), BF16),
                pltpu.VMEM((HID, HID), BF16),
                pltpu.SemaphoreType.DMA((7,)),
                pltpu.SemaphoreType.DMA((8,)),
                pltpu.SemaphoreType.DMA((8,)),
                pltpu.SemaphoreType.DMA((10,)),
                pltpu.SemaphoreType.DMA((10,)),
                pltpu.SemaphoreType.DMA((8,)),
                pltpu.SemaphoreType.DMA((8,)),
            ],
            compiler_params=pltpu.CompilerParams(
                collective_id=0, has_side_effects=True, vmem_limit_bytes=60 * 1024 * 1024
            ),
        )(positions, embed, counts, neighbours, w_one, bias_one[None], w_two, w_out[None])

    in_specs = (
        P(None, "gx", "gy", None),
        P("gx", "gy", None, None),
        P("gx", "gy"),
        P("gx", "gy", None),
        P(),
        P(),
        P(),
        P(),
    )
    out_specs = (P(None, "gx", "gy", None), P("gx", "gy", None))
    return jax.shard_map(body, mesh=mesh, in_specs=in_specs, out_specs=out_specs, check_vma=False)
```

time: 37.5 us -> 35.3 us (0.941)
  Pallas kernels: 34.5 us -> 32.5 us
    pallas_call x1, Pallas kernels: 34.5 us -> 32.5 us  [body(): pl.pallas_call(functools.partial(kernel, nx, ny), out_shape=(jax.ShapeDty...]
where the time goes in v2:
time: 35.3 us; the launch traced here: 35.1 us
  Pallas kernels  32.5 us (92%)
  local copies, waits for them, and re-layouts  1.95 us (6%)
  between operations  0.65 us (2%)
    pallas_call x1, Pallas kernels, body(): pl.pallas_call(functools.partial(kernel, nx, ny), out_shape=(jax.ShapeDty...  32.5 us
    unnamed x4, local copies, waits for them, and re-layouts  1.95 us

profile of v2, /device:TPU:1, one launch (start us, length us, event | category | flops | bytes accessed | tf_op | source)
XLA Modules:
  0.0 35.1 jit_solution(7421692398815426671)
XLA Ops:
  0.6 32.5 %shard_map.95 = (f32[3,2,8,128]{3,2,1,0:T(8,128)}, f32[2,8,128]{2,1,0:T(8,128)}) custom-call(f32[3,2,8,128]{3,2,1,0:T(8,128)} %pos_hbm.1, bf16[2,8,128,256]{3,2,1,0:T(8,128)(2,1)} %emb_hbm.1, s32[2,8]{1,0:T(2,128)} %cnt.1, s32[2,8,9]{2,1,0:T(8,128)} %nbr.1, bf16[256,256]{1,0:T(8,128)(2,1)} %w1_hbm.1, f32[1,256]{1,0:T(1,128)} %bitcast.2, ...), custom_call_target="tpu_custom_call" | custom-call | tf_op jit(solution)/shard_map/pallas_call | solution.py:326
  33.2 0.0 copy-start
  33.2 1.4 %copy.12 = f32[3,2,8,128]{3,2,1,0:T(8,128)} copy(f32[3,2,8,128]{3,2,1,0:T(8,128)} %get-tuple-element.4) | data formatting | bytes 49152
  34.5 0.0 copy-done
  34.5 0.6 %copy.13 = f32[2,8,128]{2,1,0:T(8,128)} copy(f32[2,8,128]{2,1,0:T(8,128)S(1)} %copy-done) | data formatting | bytes 16384
Async XLA Ops:
  33.2 1.4 %copy-start = (f32[2,8,128]{2,1,0:T(8,128)S(1)}, f32[2,8,128]{2,1,0:T(8,128)}, u32[]{:S(2)}) copy-start(f32[2,8,128]{2,1,0:T(8,128)} %get-tuple-element.5) | copy-start | bytes 24580

commit v3 on v2

--- a/solution.py
+++ b/solution.py
@@ -37,10 +37,10 @@
 
 def kernel(
     nx, ny,
-    pos_hbm, emb_hbm, cnt, nbr, w1_hbm, b1_hbm, w2_hbm, wo_hbm,
-    f_out, e_out,
-    emb, emb_t, raw, glob, rows, cols, weight, feat, act, grad, sums, ghost_f, recv_f,
-    pos, w1, b1, w2, wo, w1_t, w2_t,
+    pos_hbm, emb_hbm, cnt_hbm, nbr_hbm, w1_hbm, b1_hbm, w2_hbm, wo_hbm,
+    out,
+    emb, emb_t, raw, glob, rows, cols, w_mid, w_side, feat, act, grad, sums, ghost_f, recv_f,
+    pos, cnt, nbr, w1, b1, w2, wo, w1_t, w2_t,
     local_sem, p_send, p_recv, e_send, e_recv, f_send, f_recv,
 ):
     gx, gy = lax.axis_index("gx"), lax.axis_index("gy")
@@ -60,12 +60,14 @@
 
     loads = [
         pltpu.make_async_copy(pos_hbm, pos, local_sem.at[0]),
+        pltpu.make_async_copy(cnt_hbm, cnt, local_sem.at[7]),
         pltpu.make_async_copy(emb_hbm.at[home(0)], emb.at[1, pl.ds(1, BY)], local_sem.at[1]),
         pltpu.make_async_copy(emb_hbm.at[home(1)], emb.at[2, pl.ds(1, BY)], local_sem.at[6]),
         pltpu.make_async_copy(w1_hbm, w1, local_sem.at[2]),
         pltpu.make_async_copy(b1_hbm, b1, local_sem.at[3]),
         pltpu.make_async_copy(w2_hbm, w2, local_sem.at[4]),
         pltpu.make_async_copy(wo_hbm, wo, local_sem.at[5]),
+        pltpu.make_async_copy(nbr_hbm, nbr, local_sem.at[8]),
     ]
     for load in loads:
         load.start()
@@ -95,8 +97,8 @@
         (pl.ds(1, 1), hi, pl.ds(0, 1), hi, -1, 0),
         (pl.ds(1, 1), mid, pl.ds(0, 1), mid, -1, 0),
         (pl.ds(2, 1), all_y, pl.ds(3, 1), all_y, 1, 0),
-        (pl.ds(3, 1), lo, pl.ds(3, 1), east, 0, -1),
-        (pl.ds(3, 1), hi, pl.ds(3, 1), west, 0, 1),
+        (pl.ds(2, 1), west, pl.ds(3, 1), west, 1, 0),
+        (pl.ds(2, 1), east, pl.ds(3, 1), east, 1, 0),
         (pl.ds(0, 1), lo, pl.ds(0, 1), east, 0, -1),
         (pl.ds(0, 1), hi, pl.ds(0, 1), west, 0, 1),
     )
@@ -116,6 +118,7 @@
             copy.wait_recv()
 
     loads[0].wait()
+    loads[1].wait()
     lane = lax.broadcasted_iota(jnp.int32, (1, ATOMS), 1)
     for x in range(BX):
         for y in range(BY):
@@ -129,9 +132,9 @@
 
     pl.semaphore_wait(barrier, len(DIRS))
     start(p_copies)
-    loads[1].wait()
+    loads[2].wait()
     start(far_edges + far_mid)
-    loads[2].wait()
+    loads[3].wait()
     start(near_in + cols_in)
 
     row = lax.broadcasted_iota(jnp.int32, (8, ATOMS), 0)
@@ -164,11 +167,51 @@
     def flip(ex, ey):
         emb_t[ex, ey] = jnp.transpose(emb[ex, ey])
 
+    loads[8].wait()
+    def spot(g):
+        return g // (BY // 2), 2 * (g % (BY // 2))
+
+    def row_block(x, y, steps, count, height=128):
+        return jnp.concatenate([rows[x + dr, y + c, 0:height] for dr in steps for c in range(count)], axis=1)
+
+    def middle_weights(g, steps):
+        x, y = spot(g)
+        left = jnp.concatenate([cols[x, y], cols[x, y + 1]], axis=0)
+        for dr in steps:
+            power = jnp.dot(left, row_block(x, y + 1, (dr,), 2), preferred_element_type=F32)
+            w_mid[g, dr] = jnp.exp2(power).astype(BF16)
+
+    def side_weights(g):
+        x, y = spot(g)
+        for b in range(2):
+            power = jnp.dot(cols[x, y + b], row_block(x, y + 3 * b, (0, 1, 2), 1), preferred_element_type=F32)
+            w_side[g, b] = jnp.exp2(power).astype(BF16)
+
+    def middle_part(g, dr):
+        x, y = spot(g)
+        block = emb[x + dr, y + 1 : y + 3].reshape(2 * ATOMS, FEAT)
+        return jnp.dot(w_mid[g, dr], block, preferred_element_type=F32)
+
+    def own_steps(g):
+        return (1, 2) if g < GROUPS // 2 else (0, 1)
+
+    def ghost_step(g):
+        return 0 if g < GROUPS // 2 else 2
+
+    def features_of(g):
+        x, y = spot(g)
+        total = act[g] + middle_part(g, ghost_step(g))
+        for b in range(2):
+            block = emb[x : x + 3, y + 3 * b].reshape(3 * ATOMS, FEAT)
+            part = jnp.dot(w_side[g, b], block, preferred_element_type=F32)
+            half = slice(b * ATOMS, (b + 1) * ATOMS)
+            feat[g, half] = (total[half] + part).astype(BF16)
+
     for x in range(BX):
         for y in range(BY):
             place, bias = make_rows(1 + x, 1 + y)
             make_cols(x, y, place, bias)
-    for load in loads[3:]:
+    for load in loads[4:8]:
         load.wait()
     w1_t[...] = jnp.transpose(w1[...])
     w2_t[...] = jnp.transpose(w2[...])
@@ -177,35 +220,11 @@
             flip(1 + x, 1 + y)
     sums[...] = jnp.zeros_like(sums)
 
-    arrive(near_in)
-    start(near_relay)
-    arrive(p_copies)
-    for ey in range(EY):
-        make_rows(EX - 1, ey)
-        make_rows(0, ey)
-    for ex in range(1, EX - 1):
-        make_rows(ex, 0)
-        make_rows(ex, EY - 1)
-
-    def spot(g):
-        return g // (BY // 2), 2 * (g % (BY // 2))
-
-    def weights_of(g):
-        x, y = spot(g)
-        left = jnp.concatenate([cols[x, y], cols[x, y + 1]], axis=0)
-        for dr in range(3):
-            right = jnp.concatenate([rows[x + dr, y + c] for c in range(4)], axis=1)
-            power = jnp.dot(left, right, preferred_element_type=F32)
-            weight[g, dr] = jnp.exp2(power).astype(BF16)
-
-    def features_of(g):
-        x, y = spot(g)
-        total = None
-        for dr in range(3):
-            block = emb[x + dr, pl.ds(y, 4)].reshape(4 * ATOMS, FEAT)
-            part = jnp.dot(weight[g, dr], block, preferred_element_type=F32)
-            total = part if total is None else total + part
-        feat[g] = total.astype(BF16)
+    for g in range(GROUPS):
+        middle_weights(g, own_steps(g))
+    for g in range(GROUPS):
+        first, second = own_steps(g)
+        act[g] = middle_part(g, first) + middle_part(g, second)
 
     out_row = wo[...]
     bias_row = b1[...]
@@ -221,7 +240,7 @@
             for b in range(2):
                 turned = jnp.transpose(halves[b * ATOMS : (b + 1) * ATOMS])
                 energy = jnp.sum(turned, axis=0, keepdims=True)
-                e_out[home(x), y + b : y + b + 1, :] = jnp.where(lane < cnt[home(x), y + b], energy, 0.0)
+                out[3 * BX + home(x), y + b : y + b + 1, :] = jnp.where(lane < cnt[home(x), y + b], energy, 0.0)
             feat[g] = (out_row * (1.0 - two * two)).astype(BF16)
         for g in groups:
             one = act[g]
@@ -230,50 +249,101 @@
         for g in groups:
             grad[g] = jnp.dot(grad[g], w1_t[...], preferred_element_type=F32).astype(BF16)
 
-    def forces_of(g, steps):
-        x, y = spot(g)
-        slope = grad[g]
-        own = jnp.concatenate([rows[x + 1, y + 1, 0:16], rows[x + 1, y + 2, 0:16]], axis=1)
-        total = None
-        for dr in steps:
-            right = jnp.concatenate([emb_t[x + dr, y + c] for c in range(4)], axis=1)
-            projected = jnp.dot(slope, right, preferred_element_type=F32)
-            strength = projected.astype(BF16) * weight[g, dr]
-            other = jnp.concatenate([rows[x + dr, y + c, 0:16] for c in range(4)], axis=1)
-            part = lax.dot_general(
-                strength, other, (((1,), (1,)), ((), ())), preferred_element_type=F32
-            )
-            total = part if total is None else total + part
-            pushed = jnp.dot(own, strength, preferred_element_type=F32)
-            for c in range(4):
-                sums[x + dr, y + c] += pushed[:, c * ATOMS : (c + 1) * ATOMS]
-        turned = jnp.transpose(total)
-        for b in range(2):
-            sums[x + 1, y + 1 + b] += turned[:, b * ATOMS : (b + 1) * ATOMS]
+    def ghost_units(g):
+        _, y = spot(g)
+        units = [(g, 0, 2, (ghost_step(g),), 1, 2)]
+        units += [(g, b, 1, (ghost_step(g),), 3 * b, 1) for b in range(2)]
+        return units + [(g, b, 1, own_steps(g), 3 * b, 1) for b in range(2) if y + 3 * b in (0, EY - 1)]
+
+    def inner_units(g):
+        _, y = spot(g)
+        units = [(g, 0, 2, (dr,), 1, 2) for dr in own_steps(g)]
+        return units + [(g, b, 1, own_steps(g), 3 * b, 1) for b in range(2) if y + 3 * b not in (0, EY - 1)]
+
+    def project(unit):
+        g, first, slots, steps, col, count = unit
+        x, y = spot(g)
+        right = jnp.concatenate([emb_t[x + dr, y + col + c] for dr in steps for c in range(count)], axis=1)
+        slope = grad[g, first * ATOMS : (first + slots) * ATOMS]
+        return jnp.dot(slope, right, preferred_element_type=F32)
+
+    def strengthen(unit):
+        g, first, slots, steps, col, count = unit
+        projected = project(unit).astype(BF16)
+        if slots == 2:
+            w_mid[g, steps[0]] = projected * w_mid[g, steps[0]]
+        else:
+            part = slice(steps[0] * ATOMS, (steps[-1] + 1) * ATOMS)
+            w_side[g, first, :, part] = projected * w_side[g, first, :, part]
+
+    def spread(unit):
+        g, first, slots, steps, col, count = unit
+        x, y = spot(g)
+        if slots == 2:
+            strength = w_mid[g, steps[0]]
+        else:
+            strength = w_side[g, first, :, steps[0] * ATOMS : (steps[-1] + 1) * ATOMS]
+        other = row_block(x, y + col, steps, count, 16)
+        part = lax.dot_general(strength, other, (((1,), (1,)), ((), ())), preferred_element_type=F32)
+        own = row_block(x, y + 1 + first, (1,), slots, 16)
+        pushed = jnp.dot(own, strength, preferred_element_type=F32)
+        spots = [(x + dr, y + col + c) for dr in steps for c in range(count)]
+        for i, (ex, ey) in enumerate(spots):
+            sums[ex, ey] += pushed[:, i * ATOMS : (i + 1) * ATOMS]
+        return part
+
+    def forces_of(units):
+        for unit in units:
+            strengthen(unit)
+        gathered = {}
+        for unit in units:
+            part = spread(unit)
+            g, first, slots = unit[:3]
+            for b in range(slots):
+                piece = part[b * ATOMS : (b + 1) * ATOMS]
+                key = (g, first + b)
+                gathered[key] = piece if key not in gathered else gathered[key] + piece
+        for (g, b), total in gathered.items():
+            x, y = spot(g)
+            sums[x + 1, y + 1 + b] += jnp.transpose(total)
 
     def force_tile(ex, ey):
         moment = sums[ex, ey, 0:8] + sums[ex, ey, 8:16]
         return (glob[ex, ey] * moment[4:5] - moment) * INV
 
     far, near = range(GROUPS // 2), range(GROUPS // 2, GROUPS)
+    arrive(p_copies[3:8])
+    for ey in range(EY):
+        make_rows(EX - 1, ey)
+    for ex in range(1, EX - 1):
+        make_rows(ex, 0)
+        make_rows(ex, EY - 1)
     for g in near:
-        weights_of(g)
+        middle_weights(g, (2,))
+        side_weights(g)
+    arrive(p_copies[0:3])
+    for ey in range(EY):
+        make_rows(0, ey)
     arrive(far_edges)
     start(far_relay)
     for g in far:
-        weights_of(g)
-
-    arrive(cols_in + near_relay)
-    for ey in range(EY):
+        middle_weights(g, (0,))
+        side_weights(g)
+    arrive(cols_in)
+    start(near_relay)
+    arrive(near_in)
+    for ey in range(1, EY - 1):
         flip(EX - 1, ey)
     for ex in range(1, EX - 1):
         flip(ex, 0)
         flip(ex, EY - 1)
+    arrive(near_relay)
+    flip(EX - 1, 0)
+    flip(EX - 1, EY - 1)
     for g in near:
         features_of(g)
     network(near)
-    for g in near:
-        forces_of(g, (2, 0, 1))
+    forces_of([unit for g in near for unit in ghost_units(g)])
     for ey in range(EY):
         ghost_f[EX - 1, ey] = force_tile(EX - 1, ey)
     start(f_copies[5:8])
@@ -284,19 +354,15 @@
     for g in far:
         features_of(g)
     network(far)
-    for g in far:
-        forces_of(g, (0,))
+    forces_of([unit for g in far for unit in ghost_units(g)])
     for ey in range(EY):
         ghost_f[0, ey] = force_tile(0, ey)
-    start(f_copies[0:3])
-    forces_of(0, (1, 2))
-    forces_of(3, (1, 2))
     for ex in range(1, EX - 1):
         ghost_f[ex, 0] = force_tile(ex, 0)
         ghost_f[ex, EY - 1] = force_tile(ex, EY - 1)
-    start(f_copies[3:5])
-    forces_of(1, (1, 2))
-    forces_of(2, (1, 2))
+    start(f_copies[0:5])
+    forces_of([unit for g in near for unit in inner_units(g)])
+    forces_of([unit for g in far for unit in inner_units(g)])
     for x in range(BX):
         for y in range(BY):
             sums[1 + x, 1 + y, 0:8] = force_tile(1 + x, 1 + y)
@@ -310,27 +376,28 @@
             if y == BY - 1:
                 tile = tile + recv_f[1 + x, EY - 1] + recv_f[outer, EY - 1]
             for c in range(3):
-                f_out[c, home(x), y : y + 1, :] = tile[c : c + 1]
+                out[c * BX + home(x), y : y + 1, :] = tile[c : c + 1]
     for copies in (p_copies, e_copies, f_copies):
         for copy in copies:
             copy.wait_send()
 
 
+def unpack(packed, forces, energies):
+    forces[...] = packed[0 : 3 * BX]
+    energies[...] = packed[3 * BX :]
+
+
 def solution(mesh):
     nx, ny = mesh.shape["gx"], mesh.shape["gy"]
 
     def body(positions, embed, counts, neighbours, w_one, bias_one, w_two, w_out):
         hbm = pl.BlockSpec(memory_space=pl.ANY)
-        smem = pl.BlockSpec(memory_space=pltpu.SMEM)
         vmem = pl.BlockSpec(memory_space=pltpu.VMEM)
-        return pl.pallas_call(
+        packed = pl.pallas_call(
             functools.partial(kernel, nx, ny),
-            out_shape=(
-                jax.ShapeDtypeStruct((3, BX, BY, ATOMS), F32),
-                jax.ShapeDtypeStruct((BX, BY, ATOMS), F32),
-            ),
-            in_specs=[hbm, hbm, smem, smem, hbm, hbm, hbm, hbm],
-            out_specs=(vmem, vmem),
+            out_shape=jax.ShapeDtypeStruct((4 * BX, BY, ATOMS), F32),
+            in_specs=[hbm] * 8,
+            out_specs=vmem,
             scratch_shapes=[
                 pltpu.VMEM((EX, EY, ATOMS, FEAT), BF16),
                 pltpu.VMEM((EX, EY, FEAT, ATOMS), BF16),
@@ -338,7 +405,8 @@
                 pltpu.VMEM((EX, EY, 8, ATOMS), F32),
                 pltpu.VMEM((EX, EY, 128, ATOMS), BF16),
                 pltpu.VMEM((BX, BY, ATOMS, 128), BF16),
-                pltpu.VMEM((GROUPS, 3, 2 * ATOMS, 4 * ATOMS), BF16),
+                pltpu.VMEM((GROUPS, 3, 2 * ATOMS, 2 * ATOMS), BF16),
+                pltpu.VMEM((GROUPS, 2, ATOMS, 3 * ATOMS), BF16),
                 pltpu.VMEM((GROUPS, 2 * ATOMS, FEAT), BF16),
                 pltpu.VMEM((GROUPS, 2 * ATOMS, HID), F32),
                 pltpu.VMEM((GROUPS, 2 * ATOMS, FEAT), BF16),
@@ -346,13 +414,15 @@
                 pltpu.VMEM((EX, EY, 8, ATOMS), F32),
                 pltpu.VMEM((EX, EY, 8, ATOMS), F32),
                 pltpu.VMEM((3, BX, BY, ATOMS), F32),
+                pltpu.SMEM((BX, BY), jnp.int32),
+                pltpu.SMEM((BX, BY, 9), jnp.int32),
                 pltpu.VMEM((FEAT, HID), BF16),
                 pltpu.VMEM((1, HID), F32),
                 pltpu.VMEM((HID, HID), BF16),
                 pltpu.VMEM((1, HID), F32),
                 pltpu.VMEM((HID, FEAT), BF16),
                 pltpu.VMEM((HID, HID), BF16),
-                pltpu.SemaphoreType.DMA((7,)),
+                pltpu.SemaphoreType.DMA((9,)),
                 pltpu.SemaphoreType.DMA((8,)),
                 pltpu.SemaphoreType.DMA((8,)),
                 pltpu.SemaphoreType.DMA((10,)),
@@ -364,6 +434,16 @@
                 collective_id=0, has_side_effects=True, vmem_limit_bytes=60 * 1024 * 1024
             ),
         )(positions, embed, counts, neighbours, w_one, bias_one[None], w_two, w_out[None])
+        forces, energies = pl.pallas_call(
+            unpack,
+            out_shape=(
+                jax.ShapeDtypeStruct((3 * BX, BY, ATOMS), F32),
+                jax.ShapeDtypeStruct((BX, BY, ATOMS), F32),
+            ),
+            in_specs=[vmem],
+            out_specs=(vmem, vmem),
+        )(packed)
+        return forces.reshape(3, BX, BY, ATOMS), energies
 
     in_specs = (
         P(None, "gx", "gy", None),

time: 35.3 us -> 28.9 us (0.82)
  Pallas kernels: 32.5 us -> 28.1 us
  local copies, waits for them, and re-layouts: 1.95 us -> 0 us
    pallas_call x1 -> x2, Pallas kernels: 32.5 us -> 28.1 us  [the longest x1 26.7 us: body(): pl.pallas_call(functools.partial(kernel, nx, ny), out_shape=jax.ShapeDtyp...]
    unnamed x4 -> x0, local copies, waits for them, and re-layouts: 1.95 us -> none
where the time goes in v3:
time: 28.9 us; the launch traced here: 28.7 us
  Pallas kernels  28.1 us (97%)
  between operations  0.64 us (2%)
    pallas_call x1, Pallas kernels, body(): pl.pallas_call(functools.partial(kernel, nx, ny), out_shape=jax.ShapeDtyp...  26.7 us
    pallas_call x1, Pallas kernels, body(): pl.pallas_call(unpack, out_shape=(jax.ShapeDtypeStruct((3 * BX, BY, ATOMS...  1.37 us

profile of v3, /device:TPU:1, one launch (start us, length us, event | category | flops | bytes accessed | tf_op | source)
XLA Modules:
  0.0 28.7 jit_solution(4666281599617602037)
XLA Ops:
  0.6 26.7 %shard_map.95.packed = f32[8,8,128]{2,1,0:T(8,128)} custom-call(f32[3,2,8,128]{3,2,1,0:T(8,128)} %pos_hbm.1, bf16[2,8,128,256]{3,2,1,0:T(8,128)(2,1)} %emb_hbm.1, s32[2,8]{1,0:T(2,128)} %cnt_hbm.1, s32[2,8,9]{2,1,0:T(8,128)} %nbr_hbm.1, bf16[256,256]{1,0:T(8,128)(2,1)} %w1_hbm.1, f32[1,256]{1,0:T(1,128)} %bitcast.3, bf16[256,256]{1,0:T(8,128)(2,1)} %w2_hbm.1, ...), custom_call_target="tpu_custom_call" | custom-call | tf_op jit(solution)/shard_map/pallas_call | solution.py:396
  27.4 1.4 %shard_map.96 = (f32[6,8,128]{2,1,0:T(8,128)}, f32[2,8,128]{2,1,0:T(8,128)}) custom-call(f32[8,8,128]{2,1,0:T(8,128)} %shard_map.95.packed), custom_call_target="tpu_custom_call" | custom-call | tf_op jit(solution)/shard_map/pallas_call | solution.py:437

commit v4 on v3

--- a/solution.py
+++ b/solution.py
@@ -88,26 +88,33 @@
              f_send, f_recv, i, peer(side, dy))
         for i, (side, dy) in enumerate(DIRS)
     ]
-    lo, hi, mid, all_y, both = pl.ds(1, 1), pl.ds(BY, 1), pl.ds(2, BY - 2), pl.ds(1, BY), pl.ds(1, BX)
+    lo, hi, all_y = pl.ds(1, 1), pl.ds(BY, 1), pl.ds(1, BY)
     west, east = pl.ds(0, 1), pl.ds(BY + 1, 1)
+    r0, r1, r2, r3 = (pl.ds(i, 1) for i in range(EX))
     routes = (
-        (both, lo, both, east, 0, -1),
-        (both, hi, both, west, 0, 1),
-        (pl.ds(1, 1), lo, pl.ds(0, 1), lo, -1, 0),
-        (pl.ds(1, 1), hi, pl.ds(0, 1), hi, -1, 0),
-        (pl.ds(1, 1), mid, pl.ds(0, 1), mid, -1, 0),
-        (pl.ds(2, 1), all_y, pl.ds(3, 1), all_y, 1, 0),
-        (pl.ds(2, 1), west, pl.ds(3, 1), west, 1, 0),
-        (pl.ds(2, 1), east, pl.ds(3, 1), east, 1, 0),
-        (pl.ds(0, 1), lo, pl.ds(0, 1), east, 0, -1),
-        (pl.ds(0, 1), hi, pl.ds(0, 1), west, 0, 1),
+        (r2, lo, r2, east, 0, -1),
+        (r2, hi, r2, west, 0, 1),
+        (r1, lo, r1, east, 0, -1),
+        (r1, hi, r1, west, 0, 1),
+        (r1, lo, r0, lo, -1, 0),
+        (r1, hi, r0, hi, -1, 0),
+        (r1, pl.ds(2, 2), r0, pl.ds(2, 2), -1, 0),
+        (r1, pl.ds(BY - 2, 2), r0, pl.ds(BY - 2, 2), -1, 0),
+        (r1, pl.ds(4, BY - 6), r0, pl.ds(4, BY - 6), -1, 0),
+        (r2, all_y, r3, all_y, 1, 0),
+        (r2, west, r3, west, 1, 0),
+        (r2, east, r3, east, 1, 0),
+        (r0, lo, r0, east, 0, -1),
+        (r0, hi, r0, west, 0, 1),
     )
     e_copies = [
         send(emb.at[sx, sy], emb.at[tx, ty], e_send, e_recv, i, peer(side, dy))
         for i, (sx, sy, tx, ty, side, dy) in enumerate(routes)
     ]
-    cols_in, far_edges, far_mid, near_in = e_copies[0:2], e_copies[2:4], e_copies[4:5], e_copies[5:6]
-    near_relay, far_relay = e_copies[6:8], e_copies[8:10]
+    near_cols, far_cols, far_edges, far_outer, far_inner, near_in = (
+        e_copies[i:j] for i, j in ((0, 2), (2, 4), (4, 6), (6, 8), (8, 9), (9, 10))
+    )
+    near_relay, far_relay = e_copies[10:12], e_copies[12:14]
 
     def start(copies):
         for copy in copies:
@@ -133,9 +140,8 @@
     pl.semaphore_wait(barrier, len(DIRS))
     start(p_copies)
     loads[2].wait()
-    start(far_edges + far_mid)
     loads[3].wait()
-    start(near_in + cols_in)
+    start(near_cols + far_edges + near_in + far_cols + far_outer + far_inner)
 
     row = lax.broadcasted_iota(jnp.int32, (8, ATOMS), 0)
     mark = lax.broadcasted_iota(jnp.int32, (80, ATOMS), 0)
@@ -181,11 +187,24 @@
             power = jnp.dot(left, row_block(x, y + 1, (dr,), 2), preferred_element_type=F32)
             w_mid[g, dr] = jnp.exp2(power).astype(BF16)
 
-    def side_weights(g):
-        x, y = spot(g)
+    def inner_sides(g):
+        _, y = spot(g)
+        return [b for b in range(2) if y + 3 * b not in (0, EY - 1)]
+
+    def side_weights(g, b, steps):
+        x, y = spot(g)
+        power = jnp.dot(cols[x, y + b], row_block(x, y + 3 * b, steps, 1), preferred_element_type=F32)
+        w_side[g, b, :, steps[0] * ATOMS : (steps[-1] + 1) * ATOMS] = jnp.exp2(power).astype(BF16)
+
+    def late_sides(g):
         for b in range(2):
-            power = jnp.dot(cols[x, y + b], row_block(x, y + 3 * b, (0, 1, 2), 1), preferred_element_type=F32)
-            w_side[g, b] = jnp.exp2(power).astype(BF16)
+            side_weights(g, b, (ghost_step(g),) if b in inner_sides(g) else (0, 1, 2))
+
+    def side_part(g, b, steps):
+        x, y = spot(g)
+        block = emb[x + steps[0] : x + steps[-1] + 1, y + 3 * b].reshape(len(steps) * ATOMS, FEAT)
+        share = w_side[g, b, :, steps[0] * ATOMS : (steps[-1] + 1) * ATOMS]
+        return jnp.dot(share, block, preferred_element_type=F32)
 
     def middle_part(g, dr):
         x, y = spot(g)
@@ -199,11 +218,9 @@
         return 0 if g < GROUPS // 2 else 2
 
     def features_of(g):
-        x, y = spot(g)
         total = act[g] + middle_part(g, ghost_step(g))
         for b in range(2):
-            block = emb[x : x + 3, y + 3 * b].reshape(3 * ATOMS, FEAT)
-            part = jnp.dot(w_side[g, b], block, preferred_element_type=F32)
+            part = side_part(g, b, (ghost_step(g),) if b in inner_sides(g) else (0, 1, 2))
             half = slice(b * ATOMS, (b + 1) * ATOMS)
             feat[g, half] = (total[half] + part).astype(BF16)
 
@@ -222,9 +239,15 @@
 
     for g in range(GROUPS):
         middle_weights(g, own_steps(g))
+        for b in inner_sides(g):
+            side_weights(g, b, own_steps(g))
     for g in range(GROUPS):
         first, second = own_steps(g)
-        act[g] = middle_part(g, first) + middle_part(g, second)
+        total = middle_part(g, first) + middle_part(g, second)
+        for b in range(2):
+            half = slice(b * ATOMS, (b + 1) * ATOMS)
+            inner = b in inner_sides(g)
+            act[g, half] = total[half] + side_part(g, b, own_steps(g)) if inner else total[half]
 
     out_row = wo[...]
     bias_row = b1[...]
@@ -320,47 +343,59 @@
         make_rows(ex, EY - 1)
     for g in near:
         middle_weights(g, (2,))
-        side_weights(g)
+        late_sides(g)
+    arrive(near_cols)
+    start(near_relay)
     arrive(p_copies[0:3])
     for ey in range(EY):
         make_rows(0, ey)
     arrive(far_edges)
     start(far_relay)
-    for g in far:
-        middle_weights(g, (0,))
-        side_weights(g)
-    arrive(cols_in)
-    start(near_relay)
     arrive(near_in)
     for ey in range(1, EY - 1):
         flip(EX - 1, ey)
+    inside, outside = (5, 6), (4, 7)
+    for g in inside:
+        features_of(g)
+    network(inside)
+    for g in far:
+        middle_weights(g, (0,))
+        late_sides(g)
+    arrive(far_cols + near_relay)
     for ex in range(1, EX - 1):
         flip(ex, 0)
         flip(ex, EY - 1)
-    arrive(near_relay)
     flip(EX - 1, 0)
     flip(EX - 1, EY - 1)
-    for g in near:
+    for g in outside:
         features_of(g)
-    network(near)
-    forces_of([unit for g in near for unit in ghost_units(g)])
+    network(outside)
+    forces_of([unit for g in inside + outside for unit in ghost_units(g)])
     for ey in range(EY):
         ghost_f[EX - 1, ey] = force_tile(EX - 1, ey)
     start(f_copies[5:8])
 
-    arrive(far_mid + far_relay)
-    for ey in range(EY):
+    arrive(far_outer + far_relay)
+    for ey in (0, 1, 2, 3, 6, 7, 8, 9):
         flip(0, ey)
-    for g in far:
+    for g in (0, 3):
         features_of(g)
-    network(far)
-    forces_of([unit for g in far for unit in ghost_units(g)])
-    for ey in range(EY):
+    network((0, 3))
+    forces_of([unit for g in (0, 3) for unit in ghost_units(g)])
+    for ey in (0, EY - 1):
+        for ex in range(EX - 1):
+            ghost_f[ex, ey] = force_tile(ex, ey)
+    start(f_copies[1:5])
+    arrive(far_inner)
+    for ey in (4, 5):
+        flip(0, ey)
+    for g in (1, 2):
+        features_of(g)
+    network((1, 2))
+    forces_of([unit for g in (1, 2) for unit in ghost_units(g)])
+    for ey in range(1, EY - 1):
         ghost_f[0, ey] = force_tile(0, ey)
-    for ex in range(1, EX - 1):
-        ghost_f[ex, 0] = force_tile(ex, 0)
-        ghost_f[ex, EY - 1] = force_tile(ex, EY - 1)
-    start(f_copies[0:5])
+    start(f_copies[0:1])
     forces_of([unit for g in near for unit in inner_units(g)])
     forces_of([unit for g in far for unit in inner_units(g)])
     for x in range(BX):
@@ -425,8 +460,8 @@
                 pltpu.SemaphoreType.DMA((9,)),
                 pltpu.SemaphoreType.DMA((8,)),
                 pltpu.SemaphoreType.DMA((8,)),
-                pltpu.SemaphoreType.DMA((10,)),
-                pltpu.SemaphoreType.DMA((10,)),
+                pltpu.SemaphoreType.DMA((14,)),
+                pltpu.SemaphoreType.DMA((14,)),
                 pltpu.SemaphoreType.DMA((8,)),
                 pltpu.SemaphoreType.DMA((8,)),
             ],

time: 28.9 us -> 28.2 us (0.976)
  Pallas kernels: 28.1 us -> 27.4 us
    pallas_call x1, Pallas kernels: 26.7 us -> 26 us  [body(): pl.pallas_call(functools.partial(kernel, nx, ny), out_shape=jax.ShapeDtyp...]
where the time goes in v4:
time: 28.2 us; the launch traced here: 28 us
  Pallas kernels  27.4 us (97%)
  between operations  0.64 us (2%)
    pallas_call x1, Pallas kernels, body(): pl.pallas_call(functools.partial(kernel, nx, ny), out_shape=jax.ShapeDtyp...  26 us
    pallas_call x1, Pallas kernels, body(): pl.pallas_call(unpack, out_shape=(jax.ShapeDtypeStruct((3 * BX, BY, ATOMS...  1.37 us

profile of v4, /device:TPU:1, one launch (start us, length us, event | category | flops | bytes accessed | tf_op | source)
XLA Modules:
  0.0 28.0 jit_solution(5297959724837465503)
XLA Ops:
  0.6 26.0 %shard_map.95.packed = f32[8,8,128]{2,1,0:T(8,128)} custom-call(f32[3,2,8,128]{3,2,1,0:T(8,128)} %pos_hbm.1, bf16[2,8,128,256]{3,2,1,0:T(8,128)(2,1)} %emb_hbm.1, s32[2,8]{1,0:T(2,128)} %cnt_hbm.1, s32[2,8,9]{2,1,0:T(8,128)} %nbr_hbm.1, bf16[256,256]{1,0:T(8,128)(2,1)} %w1_hbm.1, f32[1,256]{1,0:T(1,128)} %bitcast.3, bf16[256,256]{1,0:T(8,128)(2,1)} %w2_hbm.1, ...), custom_call_target="tpu_custom_call" | custom-call | tf_op jit(solution)/shard_map/pallas_call | solution.py:431
  26.7 1.4 %shard_map.96 = (f32[6,8,128]{2,1,0:T(8,128)}, f32[2,8,128]{2,1,0:T(8,128)}) custom-call(f32[8,8,128]{2,1,0:T(8,128)} %shard_map.95.packed), custom_call_target="tpu_custom_call" | custom-call | tf_op jit(solution)/shard_map/pallas_call | solution.py:472

commit v5 on v4

--- a/solution.py
+++ b/solution.py
@@ -430,7 +430,7 @@
         vmem = pl.BlockSpec(memory_space=pltpu.VMEM)
         packed = pl.pallas_call(
             functools.partial(kernel, nx, ny),
-            out_shape=jax.ShapeDtypeStruct((4 * BX, BY, ATOMS), F32),
+            out_shape=pltpu.VMEM((4 * BX, BY, ATOMS), F32),
             in_specs=[hbm] * 8,
             out_specs=vmem,
             scratch_shapes=[
@@ -477,7 +477,7 @@
             ),
             in_specs=[vmem],
             out_specs=(vmem, vmem),
-        )(packed)
+        )(pltpu.with_memory_space_constraint(packed, pltpu.VMEM))
         return forces.reshape(3, BX, BY, ATOMS), energies
 
     in_specs = (

time: 28.2 us -> 26.8 us (0.950)
  Pallas kernels: 27.4 us -> 26 us
    pallas_call x1, Pallas kernels: 1.37 us -> 0.61 us  [body(): pl.pallas_call(unpack, out_shape=(jax.ShapeDtypeStruct((3 * BX, BY, ATOMS...]
    pallas_call x1, Pallas kernels: 26 us -> 25.4 us  [body(): pl.pallas_call(functools.partial(kernel, nx, ny), out_shape=pltpu.VMEM((4...]
where the time goes in v5:
time: 26.8 us; the launch traced here: 26.7 us
  Pallas kernels  26 us (97%)
  between operations  0.64 us (2%)
    pallas_call x1, Pallas kernels, body(): pl.pallas_call(functools.partial(kernel, nx, ny), out_shape=pltpu.VMEM((4...  25.4 us
    pallas_call x1, Pallas kernels, body(): pl.pallas_call(unpack, out_shape=(jax.ShapeDtypeStruct((3 * BX, BY, ATOMS...  0.61 us

profile of v5, /device:TPU:1, one launch (start us, length us, event | category | flops | bytes accessed | tf_op | source)
XLA Modules:
  0.0 26.7 jit_solution(9980361024579931229)
XLA Ops:
  0.6 25.4 %shard_map.95.packed = f32[8,8,128]{2,1,0:T(8,128)S(1)} custom-call(f32[3,2,8,128]{3,2,1,0:T(8,128)} %pos_hbm.1, bf16[2,8,128,256]{3,2,1,0:T(8,128)(2,1)} %emb_hbm.1, s32[2,8]{1,0:T(2,128)} %cnt_hbm.1, s32[2,8,9]{2,1,0:T(8,128)} %nbr_hbm.1, bf16[256,256]{1,0:T(8,128)(2,1)} %w1_hbm.1, f32[1,256]{1,0:T(1,128)} %bitcast.3, bf16[256,256]{1,0:T(8,128)(2,1)} %w2_hbm.1, ...), custom_call_target="tpu_custom_call" | custom-call | tf_op jit(solution)/shard_map/pallas_call | solution.py:431
  26.1 0.6 %shard_map.96 = (f32[6,8,128]{2,1,0:T(8,128)}, f32[2,8,128]{2,1,0:T(8,128)}) custom-call(f32[8,8,128]{2,1,0:T(8,128)S(1)} %shard_map.95.packed), custom_call_target="tpu_custom_call" | custom-call | tf_op jit(solution)/shard_map/pallas_call | solution.py:472
